TPU v7x, 32 devices: a whole 2x2x4 slice. The times are simulated.
32 devices in a mesh: pts: 8 (over z, y), var: 4 (over x, core).
Axes of the slice: x: 2, y: 2, z: 4, core: 2. Of those that a mesh axis runs over, the one named last changes fastest.
Arguments:
- tensor: bfloat16 [8, 8192, 4096], P(None, 'pts', 'var'), may hold values from -36 to 36
- level_init: float32 [64, 4096], P(None, 'var'), may hold values from -6 to 6
- time_init: float32 [8, 64], replicated, may hold values from -6 to 6
Outputs:
- point_factor: float32 [64, 8192], P(None, 'pts')
- level_factor: float32 [64, 4096], P(None, 'var')
- time_out: float32 [8, 64], replicated
All inputs are finite; a program needn't handle non-finite values.
Results may differ from a plain program's by a relative error of at most 0.011.
Values sent between devices are 32-bit elements; how exact they have to be, the bound alone decides.
No kernel may reach another device: no remote copies, remote signals or barrier semaphores. Data moves between devices by JAX's collectives and lax.ppermute only.
A program may use at most 128 MiB of HBM per device.

v0:
```python
import math

import jax
import jax.numpy as jnp
from jax import lax
from jax.sharding import PartitionSpec as P

STEPS = 8
SWEEPS = 3


HIGH_PRECISION = lax.Precision.HIGHEST
EPSILON = 1e-06


def gram_of(factor):
    return jnp.dot(factor, factor.T, precision=HIGH_PRECISION, preferred_element_type=jnp.float32)


def ridge_solve(gram_mat, right_side):
    order_count = gram_mat.shape[0]
    ridge_term = 0.01 * jnp.trace(gram_mat) / order_count + EPSILON
    system = gram_mat + ridge_term * jnp.eye(order_count, dtype=jnp.float32)
    chol_lower = jnp.linalg.cholesky(system)
    middle = lax.linalg.triangular_solve(chol_lower, right_side, left_side=True, lower=True)
    return lax.linalg.triangular_solve(
        chol_lower, middle, left_side=True, lower=True, transpose_a=True
    )


def time_products(stacked, factor):
    return jnp.sum(stacked * factor[None, :, :], axis=2)


def update_points(mttk_point, system_gram, points_all):
    share_width = mttk_point.shape[1] // lax.axis_size("var")
    summed = lax.psum(mttk_point, "var")
    solved = ridge_solve(system_gram, summed)
    share_cols = lax.dynamic_slice_in_dim(
        solved, lax.axis_index("var") * share_width, share_width, 1
    )
    whole_gram = lax.psum(gram_of(share_cols), ("pts", "var"))
    col_scale = 1.0 / jnp.sqrt(jnp.diagonal(whole_gram) / points_all + EPSILON)
    new_gram = col_scale[:, None] * whole_gram * col_scale[None, :]
    return (solved * col_scale[:, None], new_gram)


def update_levels(mttk_level, stacked, system_gram, levels_all):
    share_width = mttk_level.shape[1] // lax.axis_size("pts")
    share_start = lax.axis_index("pts") * share_width
    summed = lax.psum(mttk_level, "pts")
    solved = ridge_solve(system_gram, summed)
    share_cols = lax.dynamic_slice_in_dim(solved, share_start, share_width, 1)
    raw_time = time_products(stacked, solved)
    whole_gram, time_sum = lax.psum((gram_of(share_cols), raw_time), ("pts", "var"))
    col_scale = 1.0 / jnp.sqrt(jnp.diagonal(whole_gram) / levels_all + EPSILON)
    new_gram = col_scale[:, None] * whole_gram * col_scale[None, :]
    mttk_time = time_sum * col_scale[None, :]
    return (solved * col_scale[:, None], new_gram, mttk_time)


def per_device(tensor, level_init, time_init):
    points_all = tensor.shape[1] * lax.axis_size("pts")
    levels_all = tensor.shape[2] * lax.axis_size("var")
    level_factor = level_init
    level_grammat = lax.psum(gram_of(level_init), "var")
    time_factor = time_init
    point_factor = None
    for sweep_index in range(SWEEPS):
        time_gram = jnp.dot(
            time_factor.T, time_factor, precision=HIGH_PRECISION, preferred_element_type=jnp.float32
        )
        level_bf = level_factor.astype(jnp.bfloat16)
        mttk_point = jnp.zeros((level_factor.shape[0], tensor.shape[1]), jnp.float32)
        for step_index in range(STEPS):
            product = jnp.einsum(
                "rv,pv->rp", level_bf, tensor[step_index], preferred_element_type=jnp.float32
            )
            mttk_point = mttk_point + time_factor[step_index][:, None] * product
        point_factor, point_grammat = update_points(
            mttk_point, level_grammat * time_gram, points_all
        )
        point_bf = point_factor.astype(jnp.bfloat16)
        mttk_level = jnp.zeros((point_factor.shape[0], tensor.shape[2]), jnp.float32)
        contracted = []
        for step_index in range(STEPS):
            product = jnp.dot(point_bf, tensor[step_index], preferred_element_type=jnp.float32)
            contracted.append(product)
            mttk_level = mttk_level + time_factor[step_index][:, None] * product
        stacked = jnp.stack(contracted)
        level_factor, level_grammat, mttk_time = update_levels(
            mttk_level, stacked, point_grammat * time_gram, levels_all
        )
        time_factor = ridge_solve(point_grammat * level_grammat, mttk_time.T).T
    return (point_factor, level_factor, time_factor * math.sqrt(points_all * levels_all))


def solution(mesh):
    placed = (P(None, "pts", "var"), P(None, "var"), P())
    return jax.shard_map(
        per_device,
        mesh=mesh,
        in_specs=placed,
        out_specs=(P(None, "pts"), P(None, "var"), P()),
        check_vma=False,
    )
```

profile of v0, /device:TPU:0, one launch (start us, length us, event | category | flops | bytes accessed | tf_op | source)
XLA Modules:
  0.0 785.4 jit_solution(10724705102796187112)
XLA Ops:
  25.7 3.1 fusion.216
  29.2 12.9 %psum.112 = f32[64,64]{0,1:T(8,128)S(1)} all-reduce(f32[64,64]{0,1:T(8,128)S(1)} %fusion.380), channel_id=1, replica_groups=mesh['pts'=8,'var'=4] {'var'}, use_global_device_ids=true, to_apply=%region_0.0 | all-reduce | flops 4096 | bytes 32768 | tf_op jit(solution)/shard_map/psum | solution.py:66
  43.7 5.8 cholesky.149
  50.9 4.9 custom-call.41
  55.9 8.3 %all-reduce.10.cloned.1.call-done = f32[64,1024]{1,0:T(8,128)} async-done(((f32[64,1024]{1,0:T(8,128)}), f32[64,1024]{1,0:T(8,128)}) %all-reduce.10.cloned.1.call-update) | async-done | bytes 262160 | tf_op jit(solution)/shard_map/psum | solution.py:37
  66.1 40.0 %psum.114 = f32[64,64]{0,1:T(8,128)S(1)} all-reduce(f32[64,64]{0,1:T(8,128)S(1)} %fusion.284), channel_id=1, replica_groups=mesh['pts'=8,'var'=4] {'pts','var'}, use_global_device_ids=true, to_apply=%region_5.9 | all-reduce | flops 4096 | bytes 32768 | tf_op jit(solution)/shard_map/psum | solution.py:42
  108.5 5.8 cholesky.160
  129.7 2.9 multiply_add_fusion.2
  133.3 4.9 custom-call.43
  138.2 66.3 %all-reduce.12.cloned.1.call-done = f32[64,1024]{1,0:T(8,128)} async-done(((f32[64,1024]{1,0:T(8,128)}), f32[64,1024]{1,0:T(8,128)}) %all-reduce.12.cloned.1.call-update) | async-done | bytes 262160 | tf_op jit(solution)/shard_map/psum | solution.py:51
  206.7 40.0 %all-reduce.2 = (f32[64,64]{0,1:T(8,128)S(1)}, f32[8,64]{1,0:T(8,128)S(1)}) all-reduce(f32[64,64]{0,1:T(8,128)S(1)} %fusion.355, f32[8,64]{1,0:T(8,128)S(1)} %multiply_reduce_fusion.2), channel_id=1, replica_groups=mesh['pts'=8,'var'=4] {'pts','var'}, use_global_device_ids=true, to_apply=%region_8.12 | all-reduce | flops 4608 | bytes 36864 | tf_op jit(solution)/shard_map/psum | solution.py:55
  249.1 5.8 cholesky.171
  256.3 4.9 custom-call.45
  263.4 5.8 cholesky.182
  272.3 2.4 fusion.171
  274.6 2.4 fusion.135
  277.0 2.4 fusion.126
  279.3 2.4 fusion.111
  281.7 2.4 fusion.156
  284.1 2.4 fusion.192
  286.4 3.1 fusion.222
  290.2 4.9 custom-call.47
  295.1 26.5 %all-reduce.14.cloned.1.call-done = f32[64,1024]{1,0:T(8,128)} async-done(((f32[64,1024]{1,0:T(8,128)}), f32[64,1024]{1,0:T(8,128)}) %all-reduce.14.cloned.1.call-update) | async-done | bytes 262160 | tf_op jit(solution)/shard_map/psum | solution.py:37
  323.6 39.6 %psum.119 = f32[64,64]{0,1:T(8,128)S(1)} all-reduce(f32[64,64]{0,1:T(8,128)S(1)} %fusion.282), channel_id=1, replica_groups=mesh['pts'=8,'var'=4] {'pts','var'}, use_global_device_ids=true, to_apply=%region_14.20 | all-reduce | flops 4096 | bytes 32768 | tf_op jit(solution)/shard_map/psum | solution.py:42
  365.6 5.8 cholesky.193
  386.8 2.9 multiply_add_fusion.1
  390.4 4.9 custom-call.49
  395.4 66.3 %all-reduce.16.cloned.1.call-done = f32[64,1024]{1,0:T(8,128)} async-done(((f32[64,1024]{1,0:T(8,128)}), f32[64,1024]{1,0:T(8,128)}) %all-reduce.16.cloned.1.call-update) | async-done | bytes 262160 | tf_op jit(solution)/shard_map/psum | solution.py:51
  463.8 40.1 %all-reduce.1 = (f32[64,64]{0,1:T(8,128)S(1)}, f32[8,64]{1,0:T(8,128)S(1)}) all-reduce(f32[64,64]{0,1:T(8,128)S(1)} %fusion.353, f32[8,64]{1,0:T(8,128)S(1)} %multiply_reduce_fusion.1), channel_id=1, replica_groups=mesh['pts'=8,'var'=4] {'pts','var'}, use_global_device_ids=true, to_apply=%region_17.23 | all-reduce | flops 4608 | bytes 36864 | tf_op jit(solution)/shard_map/psum | solution.py:55
  506.4 5.8 cholesky.204
  513.6 4.9 custom-call.51
  520.6 5.8 cholesky.215
  529.5 2.4 fusion.174
  531.9 2.4 fusion.138
  536.6 2.4 fusion.120
  539.0 2.4 fusion.165
  541.3 2.4 fusion.201
  543.7 3.1 fusion.228
  547.5 4.9 custom-call.53
  552.4 26.6 %all-reduce.18.cloned.1.call-done = f32[64,1024]{1,0:T(8,128)} async-done(((f32[64,1024]{1,0:T(8,128)}), f32[64,1024]{1,0:T(8,128)}) %all-reduce.18.cloned.1.call-update) | async-done | bytes 262160 | tf_op jit(solution)/shard_map/psum | solution.py:37
  580.9 39.7 %psum.124 = f32[64,64]{0,1:T(8,128)S(1)} all-reduce(f32[64,64]{0,1:T(8,128)S(1)} %fusion.280), channel_id=1, replica_groups=mesh['pts'=8,'var'=4] {'pts','var'}, use_global_device_ids=true, to_apply=%region_23.29 | all-reduce | flops 4096 | bytes 32768 | tf_op jit(solution)/shard_map/psum | solution.py:42
  623.8 5.8 cholesky.226
  644.9 2.9 multiply_add_fusion
  648.5 4.9 custom-call.55
  653.4 66.3 %all-reduce.20.cloned.1.call-done = f32[64,1024]{1,0:T(8,128)} async-done(((f32[64,1024]{1,0:T(8,128)}), f32[64,1024]{1,0:T(8,128)}) %all-reduce.20.cloned.1.call-update) | async-done | bytes 262160 | tf_op jit(solution)/shard_map/psum | solution.py:51
  721.9 39.9 %all-reduce = (f32[64,64]{0,1:T(8,128)S(1)}, f32[8,64]{1,0:T(8,128)S(1)}) all-reduce(f32[64,64]{0,1:T(8,128)S(1)} %fusion.351, f32[8,64]{1,0:T(8,128)S(1)} %multiply_reduce_fusion), channel_id=1, replica_groups=mesh['pts'=8,'var'=4] {'pts','var'}, use_global_device_ids=true, to_apply=%region_26.32 | all-reduce | flops 4608 | bytes 36864 | tf_op jit(solution)/shard_map/psum | solution.py:55
  764.9 5.8 cholesky.237
  772.1 4.9 custom-call.57
  (164 shorter events, 111.1 us)
Async XLA Ops:
  7.2 57.0 %all-reduce.10.cloned.1.call-start = ((), (), s32[]{:S(2)}) async-start(), calls=%async_computation | async-start | bytes 524288 | tf_op jit(solution)/shard_map/psum | solution.py:37
  25.6 3.2 copy-start
  25.7 16.5 %copy-start.1 = (f32[8,64]{1,0:T(8,128)S(1)}, f32[8,64]{1,0:T(8,128)}, u32[]{:S(2)}) copy-start(f32[8,64]{1,0:T(8,128)} %param.14) | copy-start | bytes 6148
  28.8 175.7 %all-reduce.12.cloned.1.call-start = ((), (), s32[]{:S(2)}) async-start(), calls=%async_computation.1 | async-start | bytes 524288 | tf_op jit(solution)/shard_map/psum | solution.py:51
  132.6 189.1 %all-reduce.14.cloned.1.call-start = ((), (), s32[]{:S(2)}) async-start(), calls=%async_computation.2 | async-start | bytes 524288 | tf_op jit(solution)/shard_map/psum | solution.py:37
  289.5 172.2 %all-reduce.16.cloned.1.call-start = ((), (), s32[]{:S(2)}) async-start(), calls=%async_computation.3 | async-start | bytes 524288 | tf_op jit(solution)/shard_map/psum | solution.py:51
  389.7 189.2 %all-reduce.18.cloned.1.call-start = ((), (), s32[]{:S(2)}) async-start(), calls=%async_computation.4 | async-start | bytes 524288 | tf_op jit(solution)/shard_map/psum | solution.py:37
  546.8 173.0 %all-reduce.20.cloned.1.call-start = ((), (), s32[]{:S(2)}) async-start(), calls=%async_computation.5 | async-start | bytes 524288 | tf_op jit(solution)/shard_map/psum | solution.py:51
Sparse Core Ops, SparseCore 0:
  28.9 35.1 all-reduce.9
  132.7 71.8 all-reduce.11
  289.6 31.9 all-reduce.13
  389.8 71.8 all-reduce.15
  546.9 32.0 all-reduce.17
  648.0 71.7 all-reduce.19
where the time goes:
time: 793 us; the launch traced here: 785 us
  waiting for transfers between devices  260 us (33%)
  blocking collectives  252 us (32%)
  matrix products  128 us (16%)
  other arithmetic  117 us (15%)
  between operations  21.2 us (3%)
    psum x3, waiting for transfers between devices, update_levels(): summed = lax.psum(mttk_level, 'pts')  199 us
    psum x3, blocking collectives, update_levels(): lax.psum((gram_of(share_cols), raw_time), ('pts', 'var'))  120 us
    psum x3, blocking collectives, update_points(): whole_gram = lax.psum(gram_of(share_cols), ('pts', 'var'))  119 us
    psum x3, waiting for transfers between devices, update_points(): summed = lax.psum(mttk_point, 'var')  61.4 us
    dot_general x24, matrix products, per_device(): jnp.einsum('rv,pv->rp', level_bf, tensor[step_index], preferred_element_t...  58.7 us
    another operation x27, other arithmetic, ridge_solve(): chol_lower = jnp.linalg.cholesky(system)  58.7 us
    dot_general x24, matrix products, per_device(): jnp.dot(point_bf, tensor[step_index], preferred_element_type=jnp.float32)  52.4 us
    another operation x18, other arithmetic, ridge_solve(): lax.linalg.triangular_solve(chol_lower, middle, left_side=True, lower=Tru...  50 us
  transfers between devices with their start and end apart: 6, of which 6 were waited for; matrix products, arithmetic and copies ran while one was open for 5% of the time, Pallas kernels for 0%

commit v1 on v0

v1 whole, which is shorter than its diff:
```python
import functools
import math

import jax
import jax.numpy as jnp
from jax import lax
from jax.experimental import pallas as pl
from jax.experimental.pallas import tpu as pltpu
from jax.sharding import PartitionSpec as P

SWEEPS = 3
EPSILON = 1e-06
HIGHEST = lax.Precision.HIGHEST
F32 = jnp.float32
LOOK = 4


def exact_dot(a, b, dims=(((1,), (0,)), ((), ()))):
    return lax.dot_general(a, b, dims, precision=HIGHEST, preferred_element_type=F32)


NT = (((1,), (1,)), ((), ()))


def eye_mask(n):
    return lax.broadcasted_iota(jnp.int32, (n, n), 0) == lax.broadcasted_iota(jnp.int32, (n, n), 1)


def diag_row(g):
    return jnp.sum(jnp.where(eye_mask(g.shape[0]), g, 0.0), axis=0, keepdims=True)


def diag_col(g):
    return jnp.sum(jnp.where(eye_mask(g.shape[0]), g, 0.0), axis=1, keepdims=True)


def unit_scales(g, count):
    return (
        1.0 / jnp.sqrt(diag_row(g) / count + EPSILON),
        1.0 / jnp.sqrt(diag_col(g) / count + EPSILON),
    )


def with_ridge(g):
    n = g.shape[0]
    mask = eye_mask(n)
    trace = jnp.sum(jnp.sum(jnp.where(mask, g, 0.0), axis=0, keepdims=True), axis=1, keepdims=True)
    return g + jnp.where(mask, 0.01 * trace / n + EPSILON, 0.0)


def spd_inverse(a):
    n = a.shape[0]
    groups = n // 8
    wide = jnp.concatenate([a, jnp.where(eye_mask(n), 1.0, 0.0)], axis=1)
    width = 2 * n
    sub = lax.broadcasted_iota(jnp.int32, (8, width), 0)
    rows = [wide[8 * g : 8 * g + 8] for g in range(groups)]
    scale = [jnp.zeros((8, width), F32) for _ in range(groups)]
    cols = {}

    def spread(block):
        for m in range(block * LOOK, min(n, (block + 1) * LOOK)):
            cols[m] = [jnp.broadcast_to(rows[g][:, m : m + 1], (8, width)) for g in range(groups)]

    def whole(group, i):
        return jnp.broadcast_to(group[i : i + 1, :], (8, width))

    spread(0)
    for block in range(n // LOOK):
        spread(block + 1)
        for k in range(block * LOOK, (block + 1) * LOOK):
            g0, i0 = divmod(k, 8)
            col = cols.pop(k)
            inv_pivot = 1.0 / whole(col[g0], i0)
            factor = [col[g] * inv_pivot for g in range(groups)]
            factor[g0] = jnp.where(sub == i0, 0.0, factor[g0])
            scale[g0] = jnp.where(sub == i0, inv_pivot, scale[g0])
            for m in sorted(cols):
                entry = whole(col[m // 8], m % 8)
                cols[m] = [cols[m][g] - factor[g] * entry for g in range(groups)]
            pivot_row = whole(rows[g0], i0)
            rows = [rows[g] - factor[g] * pivot_row for g in range(groups)]
    return jnp.concatenate([rows[g] * scale[g] for g in range(groups)], axis=0)[:, n:]


def gram_kernel(level_ref, gram_ref):
    level = level_ref[...]
    gram_ref[...] = exact_dot(level, level, NT)


def point_pass_kernel(level_ref, tensor_ref, out_ref):
    out_ref[0] = lax.dot_general(
        level_ref[...].astype(jnp.bfloat16), tensor_ref[0], NT, preferred_element_type=F32
    )


def combine(time_cols, parts_ref, out_ref):
    total = time_cols[:, 0:1] * parts_ref[0]
    for k in range(1, parts_ref.shape[0]):
        total = total + time_cols[:, k : k + 1] * parts_ref[k]
    out_ref[...] = total


def first_combine_kernel(gram_ref, time_ref, time_cols_ref, parts_ref, out_ref, tgram_ref, system_ref):
    time = time_ref[...]
    tgram = exact_dot(time, time, (((0,), (0,)), ((), ())))
    tgram_ref[...] = tgram
    system_ref[...] = with_ridge(gram_ref[...] * tgram)
    combine(time_cols_ref[...], parts_ref, out_ref)


def combine_kernel(gram_ref, scale_ref, inverse_ref, mine_ref, other_ref, parts_ref, out_ref, tgram_ref, system_ref, time_ref):
    products = (mine_ref[...] + other_ref[...]) * scale_ref[0:1]
    inverse = inverse_ref[...]
    time = exact_dot(products, inverse)
    time_cols = exact_dot(inverse, products, NT)
    time_ref[...] = time
    tgram = exact_dot(time_cols, time_cols, NT)
    tgram_ref[...] = tgram
    system_ref[...] = with_ridge(gram_ref[...] * tgram)
    level_col = scale_ref[1:2]
    combine(time_cols * jnp.transpose(jnp.broadcast_to(level_col, (8, level_col.shape[1])))[:, 0:1], parts_ref, out_ref)


def last_time_kernel(scale_ref, inverse_ref, mine_ref, other_ref, time_ref, *, factor):
    products = (mine_ref[...] + other_ref[...]) * scale_ref[0:1]
    time_ref[...] = exact_dot(products, inverse_ref[...]) * factor


def inverse_kernel(system_ref, out_ref):
    out_ref[...] = spd_inverse(system_ref[...])


def level_pass_kernel(inverse_ref, mine_ref, other_ref, time_cols_ref, tensor_ref, solved_ref, parts_ref, lo_ref, hi_ref, rounded):
    k = pl.program_id(0)
    half = lo_ref.shape[1]

    @pl.when(k == 0)
    def _():
        solved = exact_dot(inverse_ref[...], mine_ref[...] + other_ref[...])
        solved_ref[...] = solved
        rounded[...] = solved.astype(jnp.bfloat16)
        gram = exact_dot(solved, solved, NT)
        hi_ref[:, half:] = jnp.concatenate([gram, jnp.zeros_like(gram)], axis=1)

    product = jnp.dot(rounded[...], tensor_ref[0], preferred_element_type=F32)
    parts_ref[0] = product
    weighted = time_cols_ref[0] * product

    @pl.when(k == 0)
    def _():
        lo_ref[...] = weighted[:, :half]
        hi_ref[:, :half] = weighted[:, half:]

    @pl.when(k > 0)
    def _():
        lo_ref[...] += weighted[:, :half]
        hi_ref[:, :half] += weighted[:, half:]


def level_solve_kernel(lo_ref, lo2_ref, hi_ref, hi2_ref, tgram_ref, parts_ref, solved_ref, small_ref, pgram_ref, pscale_ref, *, count):
    n = lo_ref.shape[0]
    half = lo_ref.shape[1]
    raw = hi_ref[:, half : half + n] + hi2_ref[:, half : half + n]
    row, col = unit_scales(raw, count)
    pgram = col * raw * row
    pgram_ref[...] = pgram
    pscale_ref[...] = jnp.concatenate([row, jnp.transpose(jnp.broadcast_to(col, (n, n)))[0:1]], axis=0)
    weights = spd_inverse(with_ridge(pgram * tgram_ref[...])) * row
    solved_ref[:, :half] = exact_dot(weights, lo_ref[...] + lo2_ref[...])
    solved_ref[:, half:] = exact_dot(weights, hi_ref[:, :half] + hi2_ref[:, :half])
    solved = solved_ref[...]
    small_ref[0:n] = exact_dot(solved, solved, NT)
    for k in range(parts_ref.shape[0]):
        col_sum = jnp.sum(parts_ref[k] * solved, axis=1, keepdims=True)
        small_ref[n + k : n + k + 1] = jnp.transpose(jnp.broadcast_to(col_sum, (n, n)))[0:1]


def time_inverse_kernel(small_ref, small2_ref, pgram_ref, pscale_ref, gram_ref, scale_ref, inverse_ref, products_ref, *, count):
    n = pgram_ref.shape[0]
    raw = small_ref[0:n] + small2_ref[0:n]
    row, col = unit_scales(raw, count)
    gram = col * raw * row
    gram_ref[...] = gram
    scale_ref[...] = jnp.concatenate([row * pscale_ref[0:1], row], axis=0)
    products_ref[...] = small_ref[n:] + small2_ref[n:]
    inverse_ref[...] = spd_inverse(with_ridge(pgram_ref[...] * gram))


def shape(*dims):
    return jax.ShapeDtypeStruct(dims, F32)


def call(kernel, outs, *args, name, flops=10**6):
    return pl.pallas_call(
        kernel,
        out_shape=outs,
        name=name,
        cost_estimate=pl.CostEstimate(flops=flops, bytes_accessed=10**6, transcendentals=0),
        compiler_params=pltpu.CompilerParams(vmem_limit_bytes=24 << 20),
    )(*args)


def swap(x, axis, mask):
    n = lax.axis_size(axis)
    return lax.ppermute(x, axis, [(i, i ^ mask) for i in range(n)])


def masks_of(n):
    return [1 << i for i in range(n.bit_length() - 1)]


def per_device(tensor, level_init, time_init):
    steps, points, levels = tensor.shape
    rank = level_init.shape[0]
    npts, nvar = lax.axis_size("pts"), lax.axis_size("var")
    points_all, levels_all = points * npts, levels * nvar
    pts_masks, var_masks = masks_of(npts), masks_of(nvar)
    flops = 2 * steps * points * levels * rank

    def sum_but_last(x, axis, masks):
        for mask in masks[:-1]:
            x = x + swap(x, axis, mask)
        return x, swap(x, axis, masks[-1])

    def point_pass(level):
        return pl.pallas_call(
            point_pass_kernel,
            grid=(steps,),
            in_specs=[
                pl.BlockSpec((rank, levels), lambda k: (0, 0)),
                pl.BlockSpec((1, points, levels), lambda k: (k, 0, 0)),
            ],
            out_specs=pl.BlockSpec((1, rank, points), lambda k: (k, 0, 0)),
            out_shape=shape(steps, rank, points),
            name="point_pass",
            cost_estimate=pl.CostEstimate(flops=flops, bytes_accessed=2 * tensor.size, transcendentals=0),
            compiler_params=pltpu.CompilerParams(vmem_limit_bytes=24 << 20),
        )(level, tensor)

    def level_pass(inverse, mine, other, time_cols):
        half = levels // 2
        return pl.pallas_call(
            level_pass_kernel,
            grid=(steps,),
            in_specs=[
                pl.BlockSpec((rank, rank), lambda k: (0, 0)),
                pl.BlockSpec((rank, points), lambda k: (0, 0)),
                pl.BlockSpec((rank, points), lambda k: (0, 0)),
                pl.BlockSpec((1, rank, 1), lambda k: (k, 0, 0)),
                pl.BlockSpec((1, points, levels), lambda k: (k, 0, 0)),
            ],
            out_specs=[
                pl.BlockSpec((rank, points), lambda k: (0, 0)),
                pl.BlockSpec((1, rank, levels), lambda k: (k, 0, 0)),
                pl.BlockSpec((rank, half), lambda k: (0, 0)),
                pl.BlockSpec((rank, half + 2 * rank), lambda k: (0, 0)),
            ],
            out_shape=[
                shape(rank, points),
                shape(steps, rank, levels),
                shape(rank, half),
                shape(rank, half + 2 * rank),
            ],
            scratch_shapes=[pltpu.VMEM((rank, points), jnp.bfloat16)],
            name="level_pass",
            cost_estimate=pl.CostEstimate(flops=flops, bytes_accessed=2 * tensor.size, transcendentals=0),
            compiler_params=pltpu.CompilerParams(vmem_limit_bytes=24 << 20),
        )(inverse, mine, other, time_cols, tensor)

    gram0 = call(gram_kernel, shape(rank, rank), level_init, name="level_gram")
    gram, gram_other = sum_but_last(gram0, "var", var_masks)
    gram = gram + gram_other
    parts = point_pass(level_init)
    time = time_init
    mine, tgram, system = call(
        first_combine_kernel,
        [shape(rank, points), shape(rank, rank), shape(rank, rank)],
        gram, time, time.T, parts,
        name="first_combine",
    )
    for sweep in range(SWEEPS):
        mine, other = sum_but_last(mine, "var", var_masks)
        inverse = call(inverse_kernel, shape(rank, rank), system, name="point_inverse", flops=10**7)
        point_solved, parts, lo, hi = level_pass(inverse, mine, other, time[:, :, None])
        order = pts_masks
        if len(pts_masks) > 2:
            flipped = [pts_masks[1], pts_masks[0]] + pts_masks[2:]
        else:
            flipped = pts_masks[::-1]
        for a, b in zip(order[:-1], flipped[:-1]):
            lo2, hi2 = swap(lo, "pts", a), swap(hi, "pts", b)
            lo, hi = lo + lo2, hi + hi2
        lo2, hi2 = swap(lo, "pts", order[-1]), swap(hi, "pts", flipped[-1])
        level_solved, small, pgram, pscale = call(
            functools.partial(level_solve_kernel, count=points_all),
            [shape(rank, levels), shape(rank + steps, rank), shape(rank, rank), shape(2, rank)],
            lo, lo2, hi, hi2, tgram, parts,
            name="level_solve",
        )
        small, small2 = sum_but_last(small, "var", var_masks)
        gram, scale, inverse, products = call(
            functools.partial(time_inverse_kernel, count=levels_all),
            [shape(rank, rank), shape(2, rank), shape(rank, rank), shape(steps, rank)],
            small, small2, pgram, pscale,
            name="time_inverse", flops=10**7,
        )
        products, products2 = sum_but_last(products, "pts", pts_masks)
        if sweep + 1 < SWEEPS:
            parts = point_pass(level_solved)
            mine, tgram, system, time = call(
                combine_kernel,
                [shape(rank, points), shape(rank, rank), shape(rank, rank), shape(steps, rank)],
                gram, scale, inverse, products, products2, parts,
                name="combine",
            )
        else:
            time_out = call(
                functools.partial(last_time_kernel, factor=math.sqrt(points_all * levels_all)),
                shape(steps, rank),
                scale, inverse, products, products2,
                name="last_time",
            )
    return (point_solved * pscale[0][:, None], level_solved * scale[1][:, None], time_out)


def solution(mesh):
    placed = (P(None, "pts", "var"), P(None, "var"), P())
    return jax.shard_map(
        per_device,
        mesh=mesh,
        in_specs=placed,
        out_specs=(P(None, "pts"), P(None, "var"), P()),
        check_vma=False,
    )
```

time: 793 us -> 225 us (0.28)
  blocking collectives: 252 us -> 0 us
  waiting for transfers between devices: 260 us -> 97.8 us
  matrix products: 128 us -> 0 us
  other arithmetic: 117 us -> 1.98 us
  Pallas kernels: 0 us -> 51.6 us
  starting transfers between devices: 0.25 us -> 47.9 us
  between operations: 21.2 us -> 0.91 us
  local copies, waits for them, and re-layouts: 6.63 us -> 24.6 us
    psum x6 -> x0, waiting for transfers between devices: 260 us -> none  [the longest x3 199 us: update_levels(): summed = lax.psum(mttk_level, 'pts')]
    psum x7 -> x0, blocking collectives: 252 us -> none  [the longest x3 120 us: update_levels(): lax.psum((gram_of(share_cols), raw_time), ('pts', 'var'))]
    dot_general x58 -> x0, matrix products: 115 us -> none  [the longest x24 58.7 us: per_device(): jnp.einsum('rv,pv->rp', level_bf, tensor[step_index], preferred_element_t...]
    another operation x45 -> x0, other arithmetic: 109 us -> none  [the longest x27 58.7 us: ridge_solve(): chol_lower = jnp.linalg.cholesky(system)]
    ppermute x0 -> x41, waiting for transfers between devices: none -> 97.8 us  [swap(): return lax.ppermute(x, axis, [(i, i ^ mask) for i in range(n)])]
    pallas_call x0 -> x20, Pallas kernels: none -> 51.6 us  [the longest x3 18.3 us: point_pass(): pl.pallas_call(point_pass_kernel, grid=(steps,), in_specs=[pl.BlockSpec((...]
    ppermute x0 -> x41, starting transfers between devices: none -> 47.9 us  [swap(): return lax.ppermute(x, axis, [(i, i ^ mask) for i in range(n)])]
    unnamed x4 -> x17, local copies, waits for them, and re-layouts: 0.01 us -> 24.1 us
  transfers between devices with their start and end apart: 6 -> 41, of which waited for: 6 -> 30; matrix products, arithmetic and copies ran while one was open for 5% -> 1% of each run, Pallas kernels for 0% -> 10%
where the time goes in v1:
time: 225 us
  waiting for transfers between devices  97.8 us (43%)
  Pallas kernels  51.6 us (23%)
  starting transfers between devices  47.9 us (21%)
  local copies, waits for them, and re-layouts  24.6 us (11%)
    ppermute x41, waiting for transfers between devices, swap(): return lax.ppermute(x, axis, [(i, i ^ mask) for i in range(n)])  97.8 us
    ppermute x41, starting transfers between devices, swap(): return lax.ppermute(x, axis, [(i, i ^ mask) for i in range(n)])  47.9 us
    unnamed x17, local copies, waits for them, and re-layouts  24.1 us
    pallas_call x3, Pallas kernels, point_pass(): pl.pallas_call(point_pass_kernel, grid=(steps,), in_specs=[pl.BlockSpec((...  18.3 us
    pallas_call x14, Pallas kernels, call(): pl.pallas_call(kernel, out_shape=outs, name=name, cost_estimate=pl.CostEs...  17.3 us
    pallas_call x3, Pallas kernels, level_pass(): pl.pallas_call(level_pass_kernel, grid=(steps,), in_specs=[pl.BlockSpec((...  16 us
  transfers between devices with their start and end apart: 41, of which 30 were waited for; matrix products, arithmetic and copies ran while one was open for 1% of the time, Pallas kernels for 10%

profile of v1, /device:TPU:0, one launch (start us, length us, event | category | flops | bytes accessed | tf_op | source)
XLA Modules:
  0.0 224.8 jit_solution(15231129555270182739)
XLA Ops:
  3.4 2.8 %collective-permute-start.1 = (f32[64,64]{1,0:T(8,128)S(1)}, f32[64,64]{1,0:T(8,128)S(1)}, u32[]{:S(2)}, u32[]{:S(2)}) collective-permute-start(f32[64,64]{1,0:T(8,128)S(1)} %add.78), channel_id=1, source_target_pairs={{0,2},{1,3},{2,0},{3,1},{4,6},{5,7},{6,4},{7,5},{8,10},{9,11},{10,... | collective-permute-start | bytes 49160 | tf_op jit(solution)/shard_map/ppermute | solution.py:206
  6.2 5.8 %copy-done = bf16[8,1024,1024]{2,1,0:T(8,128)(2,1)S(1)} copy-done((bf16[8,1024,1024]{2,1,0:T(8,128)(2,1)S(1)}, bf16[8,1024,1024]{2,1,0:T(8,128)(2,1)}, u32[]{:S(2)}) %copy-start) | copy-done | bytes 16777240
  12.0 6.1 %point_pass.3.parts_ref = f32[8,64,1024]{2,1,0:T(8,128)S(1)} custom-call(f32[64,1024]{1,0:T(8,128)S(1)} %copy-done.6, bf16[8,1024,1024]{2,1,0:T(8,128)(2,1)S(1)} %copy-done), custom_call_target="tpu_custom_call" | custom-call | flops 1073741824 | bytes 16777216 | tf_op jit(solution)/shard_map/point_pass/pallas_call | solution.py:227
  21.7 6.8 %collective-permute-done.3.other_ref = f32[64,1024]{1,0:T(8,128)S(1)} collective-permute-done((f32[64,1024]{1,0:T(8,128)S(1)}, f32[64,1024]{1,0:T(8,128)S(1)}, u32[]{:S(2)}, u32[]{:S(2)}) %collective-permute-start.3) | collective-permute-done | bytes 262176 | tf_op jit(solution)/shard_map/ppermute | solution.py:206
  28.6 5.8 %copy-done.1 = bf16[8,1024,1024]{2,1,0:T(8,128)(2,1)S(1)} copy-done((bf16[8,1024,1024]{2,1,0:T(8,128)(2,1)S(1)}, bf16[8,1024,1024]{2,1,0:T(8,128)(2,1)}, u32[]{:S(2)}) %copy-start.1) | copy-done | bytes 16777240
  34.3 5.6 %level_pass.3 = (f32[64,1024]{1,0:T(8,128)}, f32[8,64,1024]{2,1,0:T(8,128)S(1)}, f32[64,512]{1,0:T(8,128)S(1)}, f32[64,640]{1,0:T(8,128)S(1)}) custom-call(f32[64,64]{1,0:T(8,128)S(1)} %point_inverse.3.inverse_ref, f32[64,1024]{1,0:T(8,128)S(1)} %add.80.mine_ref, f32[64,1024]{1,0:T(8,128)S(1)} %collective-permute-done.3.other_ref, ...), custom_call_target="tpu_custom_call" | custom-call | flops 1073741824 | bytes 16777216 | tf_op jit(solution)/shard_map/level_pass/pallas_call | solution.py:243
  39.9 1.6 collective-permute-start.7
  43.0 2.3 %collective-permute-done.7 = f32[64,640]{1,0:T(8,128)S(1)} collective-permute-done((f32[64,640]{1,0:T(8,128)S(1)}, f32[64,640]{1,0:T(8,128)S(1)}, u32[]{:S(2)}, u32[]{:S(2)}) %collective-permute-start.7) | collective-permute-done | bytes 163872 | tf_op jit(solution)/shard_map/ppermute | solution.py:206
  45.3 1.6 collective-permute-start.8
  46.9 1.6 collective-permute-start.5
  48.6 2.1 collective-permute-done.8
  50.7 2.7 %collective-permute-start.9 = (f32[64,640]{1,0:T(8,128)S(1)}, f32[64,640]{1,0:T(8,128)S(1)}, u32[]{:S(2)}, u32[]{:S(2)}) collective-permute-start(f32[64,640]{1,0:T(8,128)S(1)} %add.84.hi_ref), channel_id=1, source_target_pairs={{0,16},{4,20},{8,24},{12,28},{16,0},{20,4},{24,8},{28,12},{1,17},{... | collective-permute-start | bytes 491528 | tf_op jit(solution)/shard_map/ppermute | solution.py:206
  53.4 2.6 %collective-permute-start.6 = (f32[64,512]{1,0:T(8,128)S(1)}, f32[64,512]{1,0:T(8,128)S(1)}, u32[]{:S(2)}, u32[]{:S(2)}) collective-permute-start(f32[64,512]{1,0:T(8,128)S(1)} %add.82.lo_ref), channel_id=1, source_target_pairs={{0,16},{4,20},{8,24},{12,28},{16,0},{20,4},{24,8},{28,12},{1,17},{... | collective-permute-start | bytes 393224 | tf_op jit(solution)/shard_map/ppermute | solution.py:206
  56.0 8.2 %collective-permute-done.6.lo2_ref = f32[64,512]{1,0:T(8,128)S(1)} collective-permute-done((f32[64,512]{1,0:T(8,128)S(1)}, f32[64,512]{1,0:T(8,128)S(1)}, u32[]{:S(2)}, u32[]{:S(2)}) %collective-permute-start.6) | collective-permute-done | bytes 131104 | tf_op jit(solution)/shard_map/ppermute | solution.py:206
  64.3 2.2 level_solve.3
  68.5 3.2 %collective-permute-done.11.small2_ref = f32[72,64]{1,0:T(8,128)S(1)} collective-permute-done((f32[72,64]{1,0:T(8,128)S(1)}, f32[72,64]{1,0:T(8,128)S(1)}, u32[]{:S(2)}, u32[]{:S(2)}) %collective-permute-start.11) | collective-permute-done | bytes 18464 | tf_op jit(solution)/shard_map/ppermute | solution.py:206
  74.7 2.1 collective-permute-done.12
  77.5 2.9 %collective-permute-done.13 = f32[8,64]{1,0:T(8,128)S(1)} collective-permute-done((f32[8,64]{1,0:T(8,128)S(1)}, f32[8,64]{1,0:T(8,128)S(1)}, u32[]{:S(2)}, u32[]{:S(2)}) %collective-permute-start.13) | collective-permute-done | bytes 2080 | tf_op jit(solution)/shard_map/ppermute | solution.py:206
  80.4 2.1 collective-permute-start.14
  82.5 6.1 %point_pass.4.parts_ref = f32[8,64,1024]{2,1,0:T(8,128)S(1)} custom-call(f32[64,1024]{1,0:T(8,128)S(1)} %get-tuple-element.60.level_ref, bf16[8,1024,1024]{2,1,0:T(8,128)(2,1)S(1)} %copy-done.2), custom_call_target="tpu_custom_call" | custom-call | flops 1073741824 | bytes 16777216 | tf_op jit(solution)/shard_map/point_pass/pallas_call | solution.py:227
  92.8 6.3 %collective-permute-done.16.other_ref = f32[64,1024]{1,0:T(8,128)S(1)} collective-permute-done((f32[64,1024]{1,0:T(8,128)S(1)}, f32[64,1024]{1,0:T(8,128)S(1)}, u32[]{:S(2)}, u32[]{:S(2)}) %collective-permute-start.16) | collective-permute-done | bytes 262176 | tf_op jit(solution)/shard_map/ppermute | solution.py:206
  99.1 5.8 %copy-done.3 = bf16[8,1024,1024]{2,1,0:T(8,128)(2,1)S(1)} copy-done((bf16[8,1024,1024]{2,1,0:T(8,128)(2,1)S(1)}, bf16[8,1024,1024]{2,1,0:T(8,128)(2,1)}, u32[]{:S(2)}) %copy-start.3) | copy-done | bytes 16777240
  104.9 5.6 %level_pass.4 = (f32[64,1024]{1,0:T(8,128)}, f32[8,64,1024]{2,1,0:T(8,128)S(1)}, f32[64,512]{1,0:T(8,128)S(1)}, f32[64,640]{1,0:T(8,128)S(1)}) custom-call(f32[64,64]{1,0:T(8,128)S(1)} %point_inverse.4.inverse_ref, f32[64,1024]{1,0:T(8,128)S(1)} %add.88.mine_ref, f32[64,1024]{1,0:T(8,128)S(1)} %collective-permute-done.16.other_ref, ...), custom_call_target="tpu_custom_call" | custom-call | flops 1073741824 | bytes 16777216 | tf_op jit(solution)/shard_map/level_pass/pallas_call | solution.py:243
  110.5 2.0 collective-permute-start.20
  114.0 2.2 collective-permute-done.20
  116.1 1.6 collective-permute-start.21
  117.7 1.8 collective-permute-start.18
  119.5 2.0 collective-permute-done.21
  124.6 10.7 %collective-permute-done.19.lo2_ref = f32[64,512]{1,0:T(8,128)S(1)} collective-permute-done((f32[64,512]{1,0:T(8,128)S(1)}, f32[64,512]{1,0:T(8,128)S(1)}, u32[]{:S(2)}, u32[]{:S(2)}) %collective-permute-start.19) | collective-permute-done | bytes 131104 | tf_op jit(solution)/shard_map/ppermute | solution.py:206
  135.3 2.2 level_solve.4
  139.3 3.4 %collective-permute-done.24.small2_ref = f32[72,64]{1,0:T(8,128)S(1)} collective-permute-done((f32[72,64]{1,0:T(8,128)S(1)}, f32[72,64]{1,0:T(8,128)S(1)}, u32[]{:S(2)}, u32[]{:S(2)}) %collective-permute-start.24) | collective-permute-done | bytes 18464 | tf_op jit(solution)/shard_map/ppermute | solution.py:206
  145.7 2.1 collective-permute-done.25
  147.9 3.6 %collective-permute-done.26 = f32[8,64]{1,0:T(8,128)S(1)} collective-permute-done((f32[8,64]{1,0:T(8,128)S(1)}, f32[8,64]{1,0:T(8,128)S(1)}, u32[]{:S(2)}, u32[]{:S(2)}) %collective-permute-start.26) | collective-permute-done | bytes 2080 | tf_op jit(solution)/shard_map/ppermute | solution.py:206
  151.5 6.1 %point_pass.5.parts_ref = f32[8,64,1024]{2,1,0:T(8,128)S(1)} custom-call(f32[64,1024]{1,0:T(8,128)S(1)} %get-tuple-element.75.level_ref, bf16[8,1024,1024]{2,1,0:T(8,128)(2,1)S(1)} %copy-done.4), custom_call_target="tpu_custom_call" | custom-call | flops 1073741824 | bytes 16777216 | tf_op jit(solution)/shard_map/point_pass/pallas_call | solution.py:227
  161.8 6.3 %collective-permute-done.29.other_ref = f32[64,1024]{1,0:T(8,128)S(1)} collective-permute-done((f32[64,1024]{1,0:T(8,128)S(1)}, f32[64,1024]{1,0:T(8,128)S(1)}, u32[]{:S(2)}, u32[]{:S(2)}) %collective-permute-start.29) | collective-permute-done | bytes 262176 | tf_op jit(solution)/shard_map/ppermute | solution.py:206
  168.2 5.8 %copy-done.5 = bf16[8,1024,1024]{2,1,0:T(8,128)(2,1)S(1)} copy-done((bf16[8,1024,1024]{2,1,0:T(8,128)(2,1)S(1)}, bf16[8,1024,1024]{2,1,0:T(8,128)(2,1)}, u32[]{:S(2)}) %copy-start.5) | copy-done | bytes 16777240
  173.9 4.8 %level_pass.5 = (f32[64,1024]{1,0:T(8,128)S(1)}, f32[8,64,1024]{2,1,0:T(8,128)S(1)}, f32[64,512]{1,0:T(8,128)S(1)}, f32[64,640]{1,0:T(8,128)S(1)}) custom-call(f32[64,64]{1,0:T(8,128)S(1)} %point_inverse.5.inverse_ref, f32[64,1024]{1,0:T(8,128)S(1)} %add.96.mine_ref, f32[64,1024]{1,0:T(8,128)S(1)} %collective-permute-done.29.other_ref, ...), custom_call_target="tpu_custom_call" | custom-call | flops 1073741824 | bytes 16777216 | tf_op jit(solution)/shard_map/level_pass/pallas_call | solution.py:243
  178.8 1.8 collective-permute-start.33
  182.1 2.2 collective-permute-done.33
  185.8 1.8 collective-permute-start.31
  187.6 2.0 collective-permute-done.34
  189.7 3.0 %collective-permute-start.35 = (f32[64,640]{1,0:T(8,128)S(1)}, f32[64,640]{1,0:T(8,128)S(1)}, u32[]{:S(2)}, u32[]{:S(2)}) collective-permute-start(f32[64,640]{1,0:T(8,128)S(1)} %add.100.hi_ref), channel_id=1, source_target_pairs={{0,16},{4,20},{8,24},{12,28},{16,0},{20,4},{24,8},{28,12},{1,17},{... | collective-permute-start | bytes 491528 | tf_op jit(solution)/shard_map/ppermute | solution.py:206
  192.6 2.6 %collective-permute-start.32 = (f32[64,512]{1,0:T(8,128)S(1)}, f32[64,512]{1,0:T(8,128)S(1)}, u32[]{:S(2)}, u32[]{:S(2)}) collective-permute-start(f32[64,512]{1,0:T(8,128)S(1)} %add.98.lo_ref), channel_id=1, source_target_pairs={{0,16},{4,20},{8,24},{12,28},{16,0},{20,4},{24,8},{28,12},{1,17},{... | collective-permute-start | bytes 393224 | tf_op jit(solution)/shard_map/ppermute | solution.py:206
  195.2 8.1 %collective-permute-done.32.lo2_ref = f32[64,512]{1,0:T(8,128)S(1)} collective-permute-done((f32[64,512]{1,0:T(8,128)S(1)}, f32[64,512]{1,0:T(8,128)S(1)}, u32[]{:S(2)}, u32[]{:S(2)}) %collective-permute-start.32) | collective-permute-done | bytes 131104 | tf_op jit(solution)/shard_map/ppermute | solution.py:206
  203.4 2.2 level_solve.5
  207.4 3.4 %collective-permute-done.37.small2_ref = f32[72,64]{1,0:T(8,128)S(1)} collective-permute-done((f32[72,64]{1,0:T(8,128)S(1)}, f32[72,64]{1,0:T(8,128)S(1)}, u32[]{:S(2)}, u32[]{:S(2)}) %collective-permute-start.37) | collective-permute-done | bytes 18464 | tf_op jit(solution)/shard_map/ppermute | solution.py:206
  216.0 3.6 %collective-permute-done.39 = f32[8,64]{1,0:T(8,128)S(1)} collective-permute-done((f32[8,64]{1,0:T(8,128)S(1)}, f32[8,64]{1,0:T(8,128)S(1)}, u32[]{:S(2)}, u32[]{:S(2)}) %collective-permute-start.39) | collective-permute-done | bytes 2080 | tf_op jit(solution)/shard_map/ppermute | solution.py:206
  221.5 2.5 %collective-permute-done.40.other_ref = f32[8,64]{1,0:T(8,128)S(1)} collective-permute-done((f32[8,64]{1,0:T(8,128)S(1)}, f32[8,64]{1,0:T(8,128)S(1)}, u32[]{:S(2)}, u32[]{:S(2)}) %collective-permute-start.40) | collective-permute-done | bytes 2080 | tf_op jit(solution)/shard_map/ppermute | solution.py:206
  (104 shorter events, 44.2 us)
Async XLA Ops:
  1.9 1.4 collective-permute-start
  3.4 14.8 %collective-permute-start.1 = (f32[64,64]{1,0:T(8,128)S(1)}, f32[64,64]{1,0:T(8,128)S(1)}, u32[]{:S(2)}, u32[]{:S(2)}) collective-permute-start(f32[64,64]{1,0:T(8,128)S(1)} %add.78), channel_id=1, source_target_pairs={{0,2},{1,3},{2,0},{3,1},{4,6},{5,7},{6,4},{7,5},{8,10},{9,11},{10,... | collective-permute-start | bytes 49160 | tf_op jit(solution)/shard_map/ppermute | solution.py:206
  6.2 5.8 %copy-start = (bf16[8,1024,1024]{2,1,0:T(8,128)(2,1)S(1)}, bf16[8,1024,1024]{2,1,0:T(8,128)(2,1)}, u32[]{:S(2)}) copy-start(bf16[8,1024,1024]{2,1,0:T(8,128)(2,1)} %tensor_ref.11) | copy-start | bytes 50331652
  12.0 6.1 %copy-start.7 = (f32[8,64]{1,0:T(8,128)S(1)}, f32[8,64]{1,0:T(8,128)}, u32[]{:S(2)}) copy-start(f32[8,64]{1,0:T(8,128)} %time_ref.1) | copy-start | bytes 6148
  18.5 1.6 collective-permute-start.2
  20.2 8.4 %collective-permute-start.3 = (f32[64,1024]{1,0:T(8,128)S(1)}, f32[64,1024]{1,0:T(8,128)S(1)}, u32[]{:S(2)}, u32[]{:S(2)}) collective-permute-start(f32[64,1024]{1,0:T(8,128)S(1)} %add.80.mine_ref), channel_id=1, source_target_pairs={{0,2},{1,3},{2,0},{3,1},{4,6},{5,7},{6,4},{7,5},{8,10},{9,11},{10,... | collective-permute-start | bytes 786440 | tf_op jit(solution)/shard_map/ppermute | solution.py:206
  28.6 5.8 %copy-start.1 = (bf16[8,1024,1024]{2,1,0:T(8,128)(2,1)S(1)}, bf16[8,1024,1024]{2,1,0:T(8,128)(2,1)}, u32[]{:S(2)}) copy-start(bf16[8,1024,1024]{2,1,0:T(8,128)(2,1)} %tensor_ref.11) | copy-start | bytes 50331652
  34.3 48.1 %copy-start.2 = (bf16[8,1024,1024]{2,1,0:T(8,128)(2,1)S(1)}, bf16[8,1024,1024]{2,1,0:T(8,128)(2,1)}, u32[]{:S(2)}) copy-start(bf16[8,1024,1024]{2,1,0:T(8,128)(2,1)} %tensor_ref.11) | copy-start | bytes 50331652
  39.9 5.4 %collective-permute-start.7 = (f32[64,640]{1,0:T(8,128)S(1)}, f32[64,640]{1,0:T(8,128)S(1)}, u32[]{:S(2)}, u32[]{:S(2)}) collective-permute-start(f32[64,640]{1,0:T(8,128)S(1)} %get-tuple-element.50), channel_id=1, source_target_pairs={{0,8},{4,12},{8,0},{12,4},{16,24},{20,28},{24,16},{28,20},{1,9},{5... | collective-permute-start | bytes 491528 | tf_op jit(solution)/shard_map/ppermute | solution.py:206
  41.5 5.4 %collective-permute-start.4 = (f32[64,512]{1,0:T(8,128)S(1)}, f32[64,512]{1,0:T(8,128)S(1)}, u32[]{:S(2)}, u32[]{:S(2)}) collective-permute-start(f32[64,512]{1,0:T(8,128)S(1)} %get-tuple-element.49), channel_id=1, source_target_pairs={{0,4},{4,0},{8,12},{12,8},{16,20},{20,16},{24,28},{28,24},{1,5},{5... | collective-permute-start | bytes 393224 | tf_op jit(solution)/shard_map/ppermute | solution.py:206
  45.3 5.4 %collective-permute-start.8 = (f32[64,640]{1,0:T(8,128)S(1)}, f32[64,640]{1,0:T(8,128)S(1)}, u32[]{:S(2)}, u32[]{:S(2)}) collective-permute-start(f32[64,640]{1,0:T(8,128)S(1)} %add.83), channel_id=1, source_target_pairs={{0,4},{4,0},{8,12},{12,8},{16,20},{20,16},{24,28},{28,24},{1,5},{5... | collective-permute-start | bytes 491528 | tf_op jit(solution)/shard_map/ppermute | solution.py:206
  46.9 6.5 %collective-permute-start.5 = (f32[64,512]{1,0:T(8,128)S(1)}, f32[64,512]{1,0:T(8,128)S(1)}, u32[]{:S(2)}, u32[]{:S(2)}) collective-permute-start(f32[64,512]{1,0:T(8,128)S(1)} %add.81), channel_id=1, source_target_pairs={{0,8},{4,12},{8,0},{12,4},{16,24},{20,28},{24,16},{28,20},{1,9},{5... | collective-permute-start | bytes 393224 | tf_op jit(solution)/shard_map/ppermute | solution.py:206
  50.7 13.5 %collective-permute-start.9 = (f32[64,640]{1,0:T(8,128)S(1)}, f32[64,640]{1,0:T(8,128)S(1)}, u32[]{:S(2)}, u32[]{:S(2)}) collective-permute-start(f32[64,640]{1,0:T(8,128)S(1)} %add.84.hi_ref), channel_id=1, source_target_pairs={{0,16},{4,20},{8,24},{12,28},{16,0},{20,4},{24,8},{28,12},{1,17},{... | collective-permute-start | bytes 491528 | tf_op jit(solution)/shard_map/ppermute | solution.py:206
  53.4 10.9 %collective-permute-start.6 = (f32[64,512]{1,0:T(8,128)S(1)}, f32[64,512]{1,0:T(8,128)S(1)}, u32[]{:S(2)}, u32[]{:S(2)}) collective-permute-start(f32[64,512]{1,0:T(8,128)S(1)} %add.82.lo_ref), channel_id=1, source_target_pairs={{0,16},{4,20},{8,24},{12,28},{16,0},{20,4},{24,8},{28,12},{1,17},{... | collective-permute-start | bytes 393224 | tf_op jit(solution)/shard_map/ppermute | solution.py:206
  66.5 1.3 collective-permute-start.10
  67.8 4.0 %collective-permute-start.11 = (f32[72,64]{1,0:T(8,128)S(1)}, f32[72,64]{1,0:T(8,128)S(1)}, u32[]{:S(2)}, u32[]{:S(2)}) collective-permute-start(f32[72,64]{1,0:T(8,128)S(1)} %add.85.small_ref), channel_id=1, source_target_pairs={{0,2},{1,3},{2,0},{3,1},{4,6},{5,7},{6,4},{7,5},{8,10},{9,11},{10,... | collective-permute-start | bytes 55304 | tf_op jit(solution)/shard_map/ppermute | solution.py:206
  73.2 3.6 %collective-permute-start.12 = (f32[8,64]{1,0:T(8,128)S(1)}, f32[8,64]{1,0:T(8,128)S(1)}, u32[]{:S(2)}, u32[]{:S(2)}) collective-permute-start(f32[8,64]{1,0:T(8,128)S(1)} %get-tuple-element.59), channel_id=1, source_target_pairs={{0,4},{4,0},{8,12},{12,8},{16,20},{20,16},{24,28},{28,24},{1,5},{5... | collective-permute-start | bytes 6152 | tf_op jit(solution)/shard_map/ppermute | solution.py:206
  76.8 3.6 %collective-permute-start.13 = (f32[8,64]{1,0:T(8,128)S(1)}, f32[8,64]{1,0:T(8,128)S(1)}, u32[]{:S(2)}, u32[]{:S(2)}) collective-permute-start(f32[8,64]{1,0:T(8,128)S(1)} %add.86), channel_id=1, source_target_pairs={{0,8},{4,12},{8,0},{12,4},{16,24},{20,28},{24,16},{28,20},{1,9},{5... | collective-permute-start | bytes 6152 | tf_op jit(solution)/shard_map/ppermute | solution.py:206
  80.4 8.2 %collective-permute-start.14 = (f32[8,64]{1,0:T(8,128)S(1)}, f32[8,64]{1,0:T(8,128)S(1)}, u32[]{:S(2)}, u32[]{:S(2)}) collective-permute-start(f32[8,64]{1,0:T(8,128)S(1)} %add.87.mine_ref), channel_id=1, source_target_pairs={{0,16},{4,20},{8,24},{12,28},{16,0},{20,4},{24,8},{28,12},{1,17},{... | collective-permute-start | bytes 6152 | tf_op jit(solution)/shard_map/ppermute | solution.py:206
  89.1 1.6 collective-permute-start.15
  90.7 8.4 %collective-permute-start.16 = (f32[64,1024]{1,0:T(8,128)S(1)}, f32[64,1024]{1,0:T(8,128)S(1)}, u32[]{:S(2)}, u32[]{:S(2)}) collective-permute-start(f32[64,1024]{1,0:T(8,128)S(1)} %add.88.mine_ref), channel_id=1, source_target_pairs={{0,2},{1,3},{2,0},{3,1},{4,6},{5,7},{6,4},{7,5},{8,10},{9,11},{10,... | collective-permute-start | bytes 786440 | tf_op jit(solution)/shard_map/ppermute | solution.py:206
  99.1 5.8 %copy-start.3 = (bf16[8,1024,1024]{2,1,0:T(8,128)(2,1)S(1)}, bf16[8,1024,1024]{2,1,0:T(8,128)(2,1)}, u32[]{:S(2)}) copy-start(bf16[8,1024,1024]{2,1,0:T(8,128)(2,1)} %tensor_ref.11) | copy-start | bytes 50331652
  104.9 46.6 %copy-start.4 = (bf16[8,1024,1024]{2,1,0:T(8,128)(2,1)S(1)}, bf16[8,1024,1024]{2,1,0:T(8,128)(2,1)}, u32[]{:S(2)}) copy-start(bf16[8,1024,1024]{2,1,0:T(8,128)(2,1)} %tensor_ref.11) | copy-start | bytes 50331652
  110.5 5.7 %collective-permute-start.20 = (f32[64,640]{1,0:T(8,128)S(1)}, f32[64,640]{1,0:T(8,128)S(1)}, u32[]{:S(2)}, u32[]{:S(2)}) collective-permute-start(f32[64,640]{1,0:T(8,128)S(1)} %get-tuple-element.65), channel_id=1, source_target_pairs={{0,8},{4,12},{8,0},{12,4},{16,24},{20,28},{24,16},{28,20},{1,9},{5... | collective-permute-start | bytes 491528 | tf_op jit(solution)/shard_map/ppermute | solution.py:206
  112.5 5.2 %collective-permute-start.17 = (f32[64,512]{1,0:T(8,128)S(1)}, f32[64,512]{1,0:T(8,128)S(1)}, u32[]{:S(2)}, u32[]{:S(2)}) collective-permute-start(f32[64,512]{1,0:T(8,128)S(1)} %get-tuple-element.64), channel_id=1, source_target_pairs={{0,4},{4,0},{8,12},{12,8},{16,20},{20,16},{24,28},{28,24},{1,5},{5... | collective-permute-start | bytes 393224 | tf_op jit(solution)/shard_map/ppermute | solution.py:206
  116.1 5.4 %collective-permute-start.21 = (f32[64,640]{1,0:T(8,128)S(1)}, f32[64,640]{1,0:T(8,128)S(1)}, u32[]{:S(2)}, u32[]{:S(2)}) collective-permute-start(f32[64,640]{1,0:T(8,128)S(1)} %add.91), channel_id=1, source_target_pairs={{0,4},{4,0},{8,12},{12,8},{16,20},{20,16},{24,28},{28,24},{1,5},{5... | collective-permute-start | bytes 491528 | tf_op jit(solution)/shard_map/ppermute | solution.py:206
  117.7 5.7 %collective-permute-start.18 = (f32[64,512]{1,0:T(8,128)S(1)}, f32[64,512]{1,0:T(8,128)S(1)}, u32[]{:S(2)}, u32[]{:S(2)}) collective-permute-start(f32[64,512]{1,0:T(8,128)S(1)} %add.89), channel_id=1, source_target_pairs={{0,8},{4,12},{8,0},{12,4},{16,24},{20,28},{24,16},{28,20},{1,9},{5... | collective-permute-start | bytes 393224 | tf_op jit(solution)/shard_map/ppermute | solution.py:206
  121.6 13.8 %collective-permute-start.22 = (f32[64,640]{1,0:T(8,128)S(1)}, f32[64,640]{1,0:T(8,128)S(1)}, u32[]{:S(2)}, u32[]{:S(2)}) collective-permute-start(f32[64,640]{1,0:T(8,128)S(1)} %add.92.hi_ref), channel_id=1, source_target_pairs={{0,16},{4,20},{8,24},{12,28},{16,0},{20,4},{24,8},{28,12},{1,17},{... | collective-permute-start | bytes 491528 | tf_op jit(solution)/shard_map/ppermute | solution.py:206
  123.4 11.9 %collective-permute-start.19 = (f32[64,512]{1,0:T(8,128)S(1)}, f32[64,512]{1,0:T(8,128)S(1)}, u32[]{:S(2)}, u32[]{:S(2)}) collective-permute-start(f32[64,512]{1,0:T(8,128)S(1)} %add.90.lo_ref), channel_id=1, source_target_pairs={{0,16},{4,20},{8,24},{12,28},{16,0},{20,4},{24,8},{28,12},{1,17},{... | collective-permute-start | bytes 393224 | tf_op jit(solution)/shard_map/ppermute | solution.py:206
  137.5 1.3 collective-permute-start.23
  138.8 4.0 %collective-permute-start.24 = (f32[72,64]{1,0:T(8,128)S(1)}, f32[72,64]{1,0:T(8,128)S(1)}, u32[]{:S(2)}, u32[]{:S(2)}) collective-permute-start(f32[72,64]{1,0:T(8,128)S(1)} %add.93.small_ref), channel_id=1, source_target_pairs={{0,2},{1,3},{2,0},{3,1},{4,6},{5,7},{6,4},{7,5},{8,10},{9,11},{10,... | collective-permute-start | bytes 55304 | tf_op jit(solution)/shard_map/ppermute | solution.py:206
  144.2 3.6 %collective-permute-start.25 = (f32[8,64]{1,0:T(8,128)S(1)}, f32[8,64]{1,0:T(8,128)S(1)}, u32[]{:S(2)}, u32[]{:S(2)}) collective-permute-start(f32[8,64]{1,0:T(8,128)S(1)} %get-tuple-element.74), channel_id=1, source_target_pairs={{0,4},{4,0},{8,12},{12,8},{16,20},{20,16},{24,28},{28,24},{1,5},{5... | collective-permute-start | bytes 6152 | tf_op jit(solution)/shard_map/ppermute | solution.py:206
  147.9 3.6 %collective-permute-start.26 = (f32[8,64]{1,0:T(8,128)S(1)}, f32[8,64]{1,0:T(8,128)S(1)}, u32[]{:S(2)}, u32[]{:S(2)}) collective-permute-start(f32[8,64]{1,0:T(8,128)S(1)} %add.94), channel_id=1, source_target_pairs={{0,8},{4,12},{8,0},{12,4},{16,24},{20,28},{24,16},{28,20},{1,9},{5... | collective-permute-start | bytes 6152 | tf_op jit(solution)/shard_map/ppermute | solution.py:206
  151.5 6.1 %collective-permute-start.27 = (f32[8,64]{1,0:T(8,128)S(1)}, f32[8,64]{1,0:T(8,128)S(1)}, u32[]{:S(2)}, u32[]{:S(2)}) collective-permute-start(f32[8,64]{1,0:T(8,128)S(1)} %add.95.mine_ref), channel_id=1, source_target_pairs={{0,16},{4,20},{8,24},{12,28},{16,0},{20,4},{24,8},{28,12},{1,17},{... | collective-permute-start | bytes 6152 | tf_op jit(solution)/shard_map/ppermute | solution.py:206
  158.1 1.6 collective-permute-start.28
  159.7 8.4 %collective-permute-start.29 = (f32[64,1024]{1,0:T(8,128)S(1)}, f32[64,1024]{1,0:T(8,128)S(1)}, u32[]{:S(2)}, u32[]{:S(2)}) collective-permute-start(f32[64,1024]{1,0:T(8,128)S(1)} %add.96.mine_ref), channel_id=1, source_target_pairs={{0,2},{1,3},{2,0},{3,1},{4,6},{5,7},{6,4},{7,5},{8,10},{9,11},{10,... | collective-permute-start | bytes 786440 | tf_op jit(solution)/shard_map/ppermute | solution.py:206
  168.1 5.8 %copy-start.5 = (bf16[8,1024,1024]{2,1,0:T(8,128)(2,1)S(1)}, bf16[8,1024,1024]{2,1,0:T(8,128)(2,1)}, u32[]{:S(2)}) copy-start(bf16[8,1024,1024]{2,1,0:T(8,128)(2,1)} %tensor_ref.11) | copy-start | bytes 50331652
  178.8 5.5 %collective-permute-start.33 = (f32[64,640]{1,0:T(8,128)S(1)}, f32[64,640]{1,0:T(8,128)S(1)}, u32[]{:S(2)}, u32[]{:S(2)}) collective-permute-start(f32[64,640]{1,0:T(8,128)S(1)} %get-tuple-element.81), channel_id=1, source_target_pairs={{0,8},{4,12},{8,0},{12,4},{16,24},{20,28},{24,16},{28,20},{1,9},{5... | collective-permute-start | bytes 491528 | tf_op jit(solution)/shard_map/ppermute | solution.py:206
  180.6 5.2 %collective-permute-start.30 = (f32[64,512]{1,0:T(8,128)S(1)}, f32[64,512]{1,0:T(8,128)S(1)}, u32[]{:S(2)}, u32[]{:S(2)}) collective-permute-start(f32[64,512]{1,0:T(8,128)S(1)} %get-tuple-element.80), channel_id=1, source_target_pairs={{0,4},{4,0},{8,12},{12,8},{16,20},{20,16},{24,28},{28,24},{1,5},{5... | collective-permute-start | bytes 393224 | tf_op jit(solution)/shard_map/ppermute | solution.py:206
  184.2 5.4 %collective-permute-start.34 = (f32[64,640]{1,0:T(8,128)S(1)}, f32[64,640]{1,0:T(8,128)S(1)}, u32[]{:S(2)}, u32[]{:S(2)}) collective-permute-start(f32[64,640]{1,0:T(8,128)S(1)} %add.99), channel_id=1, source_target_pairs={{0,4},{4,0},{8,12},{12,8},{16,20},{20,16},{24,28},{28,24},{1,5},{5... | collective-permute-start | bytes 491528 | tf_op jit(solution)/shard_map/ppermute | solution.py:206
  185.8 6.8 %collective-permute-start.31 = (f32[64,512]{1,0:T(8,128)S(1)}, f32[64,512]{1,0:T(8,128)S(1)}, u32[]{:S(2)}, u32[]{:S(2)}) collective-permute-start(f32[64,512]{1,0:T(8,128)S(1)} %add.97), channel_id=1, source_target_pairs={{0,8},{4,12},{8,0},{12,4},{16,24},{20,28},{24,16},{28,20},{1,9},{5... | collective-permute-start | bytes 393224 | tf_op jit(solution)/shard_map/ppermute | solution.py:206
  189.7 13.7 %collective-permute-start.35 = (f32[64,640]{1,0:T(8,128)S(1)}, f32[64,640]{1,0:T(8,128)S(1)}, u32[]{:S(2)}, u32[]{:S(2)}) collective-permute-start(f32[64,640]{1,0:T(8,128)S(1)} %add.100.hi_ref), channel_id=1, source_target_pairs={{0,16},{4,20},{8,24},{12,28},{16,0},{20,4},{24,8},{28,12},{1,17},{... | collective-permute-start | bytes 491528 | tf_op jit(solution)/shard_map/ppermute | solution.py:206
  192.6 10.7 %collective-permute-start.32 = (f32[64,512]{1,0:T(8,128)S(1)}, f32[64,512]{1,0:T(8,128)S(1)}, u32[]{:S(2)}, u32[]{:S(2)}) collective-permute-start(f32[64,512]{1,0:T(8,128)S(1)} %add.98.lo_ref), channel_id=1, source_target_pairs={{0,16},{4,20},{8,24},{12,28},{16,0},{20,4},{24,8},{28,12},{1,17},{... | collective-permute-start | bytes 393224 | tf_op jit(solution)/shard_map/ppermute | solution.py:206
  205.6 1.3 collective-permute-start.36
  206.9 4.0 %collective-permute-start.37 = (f32[72,64]{1,0:T(8,128)S(1)}, f32[72,64]{1,0:T(8,128)S(1)}, u32[]{:S(2)}, u32[]{:S(2)}) collective-permute-start(f32[72,64]{1,0:T(8,128)S(1)} %add.101.small_ref), channel_id=1, source_target_pairs={{0,2},{1,3},{2,0},{3,1},{4,6},{5,7},{6,4},{7,5},{8,10},{9,11},{10,... | collective-permute-start | bytes 55304 | tf_op jit(solution)/shard_map/ppermute | solution.py:206
  212.3 3.7 %collective-permute-start.38 = (f32[8,64]{1,0:T(8,128)S(1)}, f32[8,64]{1,0:T(8,128)S(1)}, u32[]{:S(2)}, u32[]{:S(2)}) collective-permute-start(f32[8,64]{1,0:T(8,128)S(1)} %get-tuple-element.90), channel_id=1, source_target_pairs={{0,4},{4,0},{8,12},{12,8},{16,20},{20,16},{24,28},{28,24},{1,5},{5... | collective-permute-start | bytes 6152 | tf_op jit(solution)/shard_map/ppermute | solution.py:206
  216.0 3.6 %collective-permute-start.39 = (f32[8,64]{1,0:T(8,128)S(1)}, f32[8,64]{1,0:T(8,128)S(1)}, u32[]{:S(2)}, u32[]{:S(2)}) collective-permute-start(f32[8,64]{1,0:T(8,128)S(1)} %add.102), channel_id=1, source_target_pairs={{0,8},{4,12},{8,0},{12,4},{16,24},{20,28},{24,16},{28,20},{1,9},{5... | collective-permute-start | bytes 6152 | tf_op jit(solution)/shard_map/ppermute | solution.py:206
  219.6 4.5 %collective-permute-start.40 = (f32[8,64]{1,0:T(8,128)S(1)}, f32[8,64]{1,0:T(8,128)S(1)}, u32[]{:S(2)}, u32[]{:S(2)}) collective-permute-start(f32[8,64]{1,0:T(8,128)S(1)} %add.103.mine_ref), channel_id=1, source_target_pairs={{0,16},{4,20},{8,24},{12,28},{16,0},{20,4},{24,8},{28,12},{1,17},{... | collective-permute-start | bytes 6152 | tf_op jit(solution)/shard_map/ppermute | solution.py:206
  (1 other events, 1.0 us)

commit v2 on v1

v2 whole, which is shorter than its diff:
```python
import functools
import math

import jax
import jax.numpy as jnp
from jax import lax
from jax.experimental import pallas as pl
from jax.experimental.pallas import tpu as pltpu
from jax.sharding import PartitionSpec as P


SWEEPS = 3
EPSILON = 1e-06
HIGHEST = lax.Precision.HIGHEST
F32 = jnp.float32
LOOK = 4
PIECES = (2, 6)


def exact_dot(a, b, dims=(((1,), (0,)), ((), ()))):
    return lax.dot_general(a, b, dims, precision=HIGHEST, preferred_element_type=F32)


NT = (((1,), (1,)), ((), ()))


def eye_mask(n):
    return lax.broadcasted_iota(jnp.int32, (n, n), 0) == lax.broadcasted_iota(jnp.int32, (n, n), 1)


def diag_row(g):
    return jnp.sum(jnp.where(eye_mask(g.shape[0]), g, 0.0), axis=0, keepdims=True)


def diag_col(g):
    return jnp.sum(jnp.where(eye_mask(g.shape[0]), g, 0.0), axis=1, keepdims=True)


def unit_scales(g, count):
    return (
        1.0 / jnp.sqrt(diag_row(g) / count + EPSILON),
        1.0 / jnp.sqrt(diag_col(g) / count + EPSILON),
    )


def with_ridge(g):
    n = g.shape[0]
    mask = eye_mask(n)
    trace = jnp.sum(jnp.sum(jnp.where(mask, g, 0.0), axis=0, keepdims=True), axis=1, keepdims=True)
    return g + jnp.where(mask, 0.01 * trace / n + EPSILON, 0.0)


def spd_inverse(a):
    n = a.shape[0]
    groups = n // 8
    wide = jnp.concatenate([a, jnp.where(eye_mask(n), 1.0, 0.0)], axis=1)
    width = 2 * n
    sub = lax.broadcasted_iota(jnp.int32, (8, width), 0)
    rows = [wide[8 * g : 8 * g + 8] for g in range(groups)]
    scale = [jnp.zeros((8, width), F32) for _ in range(groups)]
    cols = {}

    def spread(block):
        for m in range(block * LOOK, min(n, (block + 1) * LOOK)):
            cols[m] = [jnp.broadcast_to(rows[g][:, m : m + 1], (8, width)) for g in range(groups)]

    def whole(group, i):
        return jnp.broadcast_to(group[i : i + 1, :], (8, width))

    spread(0)
    for block in range(n // LOOK):
        spread(block + 1)
        for k in range(block * LOOK, (block + 1) * LOOK):
            g0, i0 = divmod(k, 8)
            col = cols.pop(k)
            inv_pivot = 1.0 / whole(col[g0], i0)
            factor = [col[g] * inv_pivot for g in range(groups)]
            factor[g0] = jnp.where(sub == i0, 0.0, factor[g0])
            scale[g0] = jnp.where(sub == i0, inv_pivot, scale[g0])
            for m in sorted(cols):
                entry = whole(col[m // 8], m % 8)
                cols[m] = [cols[m][g] - factor[g] * entry for g in range(groups)]
            pivot_row = whole(rows[g0], i0)
            rows = [rows[g] - factor[g] * pivot_row for g in range(groups)]
    return jnp.concatenate([rows[g] * scale[g] for g in range(groups)], axis=0)[:, n:]


def gram_kernel(level_ref, gram_ref):
    level = level_ref[...]
    gram_ref[...] = exact_dot(level, level, NT)


def point_pass_kernel(level_ref, tensor_ref, out_ref, *, first):
    rounded = level_ref[...].astype(jnp.bfloat16)
    for k in range(out_ref.shape[0]):
        out_ref[k] = lax.dot_general(rounded, tensor_ref[first + k], NT, preferred_element_type=F32)


def combine(time_cols, parts_refs, out_ref):
    total, k = None, 0
    for parts_ref in parts_refs:
        for i in range(parts_ref.shape[0]):
            term = time_cols[:, k : k + 1] * parts_ref[i]
            total = term if total is None else total + term
            k += 1
    out_ref[...] = total


def first_combine_kernel(gram_ref, time_ref, time_cols_ref, *refs):
    *parts_refs, out_ref, tgram_ref, system_ref = refs
    time = time_ref[...]
    tgram = exact_dot(time, time, (((0,), (0,)), ((), ())))
    tgram_ref[...] = tgram
    system_ref[...] = with_ridge(gram_ref[...] * tgram)
    combine(time_cols_ref[...], parts_refs, out_ref)


def combine_kernel(gram_ref, scale_ref, inverse_ref, mine_ref, other_ref, *refs):
    *parts_refs, out_ref, tgram_ref, system_ref, time_ref = refs
    inverse = inverse_ref[...]
    products = (mine_ref[...] + other_ref[...]) * scale_ref[0:1]
    time_ref[...] = exact_dot(products, inverse)
    time_cols = exact_dot(inverse, products, NT)
    tgram = exact_dot(time_cols, time_cols, NT)
    tgram_ref[...] = tgram
    system_ref[...] = with_ridge(gram_ref[...] * tgram)
    level_row = scale_ref[1:2]
    level_col = jnp.transpose(jnp.broadcast_to(level_row, (8, level_row.shape[1])))[:, 0:1]
    combine(time_cols * level_col, parts_refs, out_ref)


def last_time_kernel(scale_ref, inverse_ref, mine_ref, other_ref, time_ref, *, factor):
    products = (mine_ref[...] + other_ref[...]) * scale_ref[0:1]
    time_ref[...] = exact_dot(products, inverse_ref[...]) * factor


def slab_copies(tensor_ref, held_ref, sems):
    copies = [pltpu.make_async_copy(tensor_ref.at[k], held_ref.at[k], sems.at[k]) for k in range(held_ref.shape[0])]
    for copy in copies:
        copy.start()
    return copies


def inverse_kernel(system_ref, tensor_ref, out_ref, held_ref, sems):
    copies = slab_copies(tensor_ref, held_ref, sems)
    out_ref[...] = spd_inverse(system_ref[...])
    for copy in copies:
        copy.wait()


def first_pass_kernel(level_ref, tensor_ref, out_ref, held, sems):
    copies = slab_copies(tensor_ref, held, sems)
    rounded = level_ref[...].astype(jnp.bfloat16)
    for k, copy in enumerate(copies):
        copy.wait()
        out_ref[k] = lax.dot_general(rounded, held[k], NT, preferred_element_type=F32)


def level_pass_kernel(
    side_ref, inverse_ref, mine_ref, other_ref, time_cols_ref, tensor_ref, solved_ref, parts_ref, keep_ref, send_ref, sums
):
    half = sums.shape[2]
    solved = exact_dot(inverse_ref[...], mine_ref[...] + other_ref[...])
    solved_ref[...] = solved
    rounded = solved.astype(jnp.bfloat16)
    gram = exact_dot(solved, solved, NT)
    gram = jnp.concatenate([gram, jnp.zeros_like(gram)], axis=1)
    keep_ref[:, half:] = gram
    send_ref[:, half:] = gram
    for k in range(tensor_ref.shape[0]):
        product = jnp.dot(rounded, tensor_ref[k], preferred_element_type=F32)
        parts_ref[k] = product
        weighted = time_cols_ref[:, k : k + 1] * product
        for i in range(2):
            piece = weighted[:, i * half : (i + 1) * half]
            sums[i] = piece if k == 0 else sums[i] + piece
    side = side_ref[0]
    keep_ref[:, :half] = sums[side]
    send_ref[:, :half] = sums[1 - side]


def level_weights_kernel(mine_ref, tgram_ref, weights_ref, pgram_ref, pscale_ref, *, count):
    n = tgram_ref.shape[0]
    half = mine_ref.shape[1] - 2 * n
    raw = mine_ref[:, half : half + n]
    row, col = unit_scales(raw, count)
    pgram = col * raw * row
    pgram_ref[...] = pgram
    pscale_ref[...] = row
    weights_ref[...] = spd_inverse(with_ridge(pgram * tgram_ref[...])) * row


def level_solve_kernel(side_ref, weights_ref, mine_ref, other_ref, parts_ref, solved_ref, small_ref):
    n = weights_ref.shape[0]
    half = solved_ref.shape[1] // 2
    side = side_ref[0]
    weights = weights_ref[...]
    solved_ref[:, pl.ds(pl.multiple_of(side * half, half), half)] = exact_dot(weights, mine_ref[:, :half])
    solved_ref[:, pl.ds(pl.multiple_of((1 - side) * half, half), half)] = exact_dot(weights, other_ref[:, :half])
    solved = solved_ref[...]
    small_ref[0:n] = exact_dot(solved, solved, NT)
    for k in range(parts_ref.shape[0]):
        col_sum = jnp.sum(parts_ref[k] * solved, axis=1, keepdims=True)
        small_ref[n + k : n + k + 1] = jnp.transpose(jnp.broadcast_to(col_sum, (n, n)))[0:1]


def time_inverse_kernel(small_ref, pgram_ref, pscale_ref, gram_ref, scale_ref, inverse_ref, *, count):
    n = pgram_ref.shape[0]
    raw = small_ref[0:n]
    row, col = unit_scales(raw, count)
    gram = col * raw * row
    gram_ref[...] = gram
    scale_ref[...] = jnp.concatenate([row * pscale_ref[...], row], axis=0)
    inverse_ref[...] = spd_inverse(with_ridge(pgram_ref[...] * gram))


def shape(*dims):
    return jax.ShapeDtypeStruct(dims, F32)


def call(kernel, outs, *args, flops=10**6, spaces=None, limit=8, scratch=()):
    spaces = spaces or [pltpu.VMEM] * len(args)
    return pl.pallas_call(
        kernel,
        out_shape=outs,
        in_specs=[pl.BlockSpec(memory_space=space) for space in spaces],
        out_specs=[pl.BlockSpec(memory_space=pltpu.VMEM)] * len(outs),
        scratch_shapes=scratch,
        cost_estimate=pl.CostEstimate(flops=flops, bytes_accessed=10**6, transcendentals=0),
        compiler_params=pltpu.CompilerParams(vmem_limit_bytes=limit << 20),
    )(*args)


def swap(x, axis, mask):
    n = lax.axis_size(axis)
    return lax.ppermute(x, axis, [(i, i ^ mask) for i in range(n)])


def masks_of(n):
    return [1 << i for i in range(n.bit_length() - 1)]


def per_device(tensor, level_init, time_init):
    steps, points, levels = tensor.shape
    rank = level_init.shape[0]
    npts, nvar = lax.axis_size("pts"), lax.axis_size("var")
    points_all, levels_all = points * npts, levels * nvar
    pts_masks, var_masks = masks_of(npts), masks_of(nvar)
    half = levels // 2
    flops = 2 * steps * points * levels * rank
    V, S = pltpu.VMEM, pltpu.SMEM
    dma_sems = pltpu.SemaphoreType.DMA((steps,))
    square = shape(rank, rank)
    tensor_hbm = pltpu.with_memory_space_constraint(tensor, pltpu.HBM)
    side = (lax.axis_index("pts") & 1).astype(jnp.int32)[None]

    def sum_over(x, axis, masks):
        for mask in masks:
            x = x + swap(x, axis, mask)
        return x

    (gram,) = call(gram_kernel, [square], level_init)
    gram = sum_over(gram, "var", var_masks)
    (first,) = call(
        first_pass_kernel, [shape(steps, rank, points)], level_init, tensor_hbm,
        flops=flops, limit=24, spaces=[V, pltpu.HBM],
        scratch=[V(tensor.shape, tensor.dtype), dma_sems],
    )
    time = time_init
    mine, tgram, system = call(first_combine_kernel, [shape(rank, points), square, square], gram, time, time.T, first)
    for sweep in range(SWEEPS):
        mine = sum_over(mine, "var", var_masks[:-1])
        other = swap(mine, "var", var_masks[-1])
        inverse, held = call(
            inverse_kernel, [square, V(tensor.shape, tensor.dtype)], system, tensor_hbm,
            flops=flops, limit=24, spaces=[V, pltpu.HBM], scratch=[dma_sems],
        )
        held = pltpu.with_memory_space_constraint(held, V)
        point_solved, parts, keep, send = call(
            level_pass_kernel,
            [shape(rank, points), shape(steps, rank, levels)] + [shape(rank, half + 2 * rank)] * 2,
            side, inverse, mine, other, time.T, held,
            flops=flops, limit=24, spaces=[S] + [V] * 5,
            scratch=[V((2, rank, half), F32)],
        )
        keep = keep + swap(send, "pts", pts_masks[0])
        keep = sum_over(keep, "pts", pts_masks[1:])
        other = swap(keep, "pts", pts_masks[0])
        weights, pgram, pscale = call(
            functools.partial(level_weights_kernel, count=points_all),
            [square, square, shape(1, rank)], keep, tgram,
            flops=10**7,
        )
        level_solved, small = call(
            level_solve_kernel, [shape(rank, levels), shape(rank + steps, rank)],
            side, weights, keep, other, parts,
            spaces=[S] + [V] * 4,
        )
        small = sum_over(small, "var", var_masks)
        products = small[rank:]
        gram, scale, inverse = call(
            functools.partial(time_inverse_kernel, count=levels_all),
            [square, shape(2, rank), square], small, pgram, pscale,
            flops=10**7,
        )
        for i, mask in enumerate(pts_masks):
            products2 = swap(products, "pts", mask)
            if i + 1 < len(pts_masks):
                products = products + products2
        if sweep + 1 < SWEEPS:
            pieces, first = [], 0
            for count in PIECES:
                pieces += call(
                    functools.partial(point_pass_kernel, first=first), [shape(count, rank, points)],
                    level_solved, held,
                    flops=flops * count // steps, limit=24,
                )
                first += count
            mine, tgram, system, time = call(
                combine_kernel, [shape(rank, points), square, square, shape(steps, rank)],
                gram, scale, inverse, products, products2, *pieces,
            )
    (time_out,) = call(
        functools.partial(last_time_kernel, factor=math.sqrt(points_all * levels_all)), [shape(steps, rank)],
        scale, inverse, products, products2,
    )
    return (point_solved * pscale[0][:, None], level_solved * scale[1][:, None], time_out)


def solution(mesh):
    placed = (P(None, "pts", "var"), P(None, "var"), P())
    return jax.shard_map(
        per_device,
        mesh=mesh,
        in_specs=placed,
        out_specs=(P(None, "pts"), P(None, "var"), P()),
        check_vma=False,
    )
```

time: 225 us -> 189 us (0.84)
  local copies, waits for them, and re-layouts: 24.6 us -> 2.17 us
  waiting for transfers between devices: 97.8 us -> 80 us
  Pallas kernels: 51.6 us -> 62.7 us
  starting transfers between devices: 47.9 us -> 40.9 us
    unnamed x17 -> x7, local copies, waits for them, and re-layouts: 24.1 us -> 1.98 us
    ppermute x41 -> x35, waiting for transfers between devices: 97.8 us -> 80 us  [swap(): return lax.ppermute(x, axis, [(i, i ^ mask) for i in range(n)])]
    pallas_call x20 -> x25, Pallas kernels: 51.6 us -> 62.7 us  [call(): pl.pallas_call(kernel, out_shape=outs, in_specs=[pl.BlockSpec(memory_spac...]
    ppermute x41 -> x35, starting transfers between devices: 47.9 us -> 40.9 us  [swap(): return lax.ppermute(x, axis, [(i, i ^ mask) for i in range(n)])]
  transfers between devices with their start and end apart: 41 -> 35, of which waited for: 30 -> 30; matrix products, arithmetic and copies ran while one was open for 1% -> 1% of each run, Pallas kernels for 10% -> 24%
where the time goes in v2:
time: 189 us
  waiting for transfers between devices  80 us (42%)
  Pallas kernels  62.7 us (33%)
  starting transfers between devices  40.9 us (22%)
  local copies, waits for them, and re-layouts  2.17 us (1%)
  other arithmetic  1.92 us (1%)
    ppermute x35, waiting for transfers between devices, swap(): return lax.ppermute(x, axis, [(i, i ^ mask) for i in range(n)])  80 us
    pallas_call x25, Pallas kernels, call(): pl.pallas_call(kernel, out_shape=outs, in_specs=[pl.BlockSpec(memory_spac...  62.7 us
    ppermute x35, starting transfers between devices, swap(): return lax.ppermute(x, axis, [(i, i ^ mask) for i in range(n)])  40.9 us
  transfers between devices with their start and end apart: 35, of which 30 were waited for; matrix products, arithmetic and copies ran while one was open for 1% of the time, Pallas kernels for 24%

profile of v2, /device:TPU:0, one launch (start us, length us, event | category | flops | bytes accessed | tf_op | source)
XLA Modules:
  0.0 188.6 jit_solution(11163531708187989381)
XLA Ops:
  3.4 2.8 %collective-permute-start.1 = (f32[64,64]{1,0:T(8,128)S(1)}, f32[64,64]{1,0:T(8,128)S(1)}, u32[]{:S(2)}, u32[]{:S(2)}) collective-permute-start(f32[64,64]{1,0:T(8,128)S(1)} %add.78), channel_id=1, source_target_pairs={{0,2},{1,3},{2,0},{3,1},{4,6},{5,7},{6,4},{7,5},{8,10},{9,11},{10,... | collective-permute-start | bytes 49160 | tf_op jit(solution)/shard_map/ppermute | solution.py:236
  7.1 7.7 %shard_map.59.refs_0_ = f32[8,64,1024]{2,1,0:T(8,128)S(1)} custom-call(f32[64,1024]{1,0:T(8,128)S(1)} %copy-done.1, bf16[8,1024,1024]{2,1,0:T(8,128)(2,1)} %tensor_ref.7), custom_call_target="tpu_custom_call" | custom-call | flops 1073741824 | bytes 1000000 | tf_op jit(solution)/shard_map/pallas_call | solution.py:223
  17.0 6.0 %shard_map.61 = (f32[64,64]{1,0:T(8,128)S(1)}, bf16[8,1024,1024]{2,1,0:T(8,128)(2,1)S(1)}) custom-call(f32[64,64]{1,0:T(8,128)S(1)} %get-tuple-element.53.system_ref, bf16[8,1024,1024]{2,1,0:T(8,128)(2,1)} %tensor_ref.7), custom_call_target="tpu_custom_call" | custom-call | flops 1073741824 | bytes 1000000 | tf_op jit(solution)/shard_map/pallas_call | solution.py:223
  23.0 2.4 %collective-permute-done.3.other_ref = f32[64,1024]{1,0:T(8,128)S(1)} collective-permute-done((f32[64,1024]{1,0:T(8,128)S(1)}, f32[64,1024]{1,0:T(8,128)S(1)}, u32[]{:S(2)}, u32[]{:S(2)}) %collective-permute-start.3) | collective-permute-done | bytes 262176 | tf_op jit(solution)/shard_map/ppermute | solution.py:236
  25.3 4.1 %shard_map.62 = (f32[64,1024]{1,0:T(8,128)}, f32[8,64,1024]{2,1,0:T(8,128)S(1)}, f32[64,640]{1,0:T(8,128)S(1)}, f32[64,640]{1,0:T(8,128)S(1)}) custom-call(s32[1]{0:T(128)} %bitcast.side_ref, f32[64,64]{1,0:T(8,128)S(1)} %get-tuple-element.54.inverse_ref, f32[64,1024]{1,0:T(8,128)S(1)} %add.80.mine_ref, f32[64,1024]{1,0:T(8,128)S(1)} %collective-permute-done.3.other_ref, ...), custom_call_target="tpu_custom_call" | custom-call | flops 1073741824 | bytes 1000000 | tf_op jit(solution)/shard_map/pallas_call | solution.py:223
  29.4 1.5 collective-permute-start.4
  31.0 3.9 %collective-permute-done.4 = f32[64,640]{1,0:T(8,128)S(1)} collective-permute-done((f32[64,640]{1,0:T(8,128)S(1)}, f32[64,640]{1,0:T(8,128)S(1)}, u32[]{:S(2)}, u32[]{:S(2)}) %collective-permute-start.4) | collective-permute-done | bytes 163872 | tf_op jit(solution)/shard_map/ppermute | solution.py:236
  34.8 1.6 collective-permute-start.5
  36.5 3.7 %collective-permute-done.5 = f32[64,640]{1,0:T(8,128)S(1)} collective-permute-done((f32[64,640]{1,0:T(8,128)S(1)}, f32[64,640]{1,0:T(8,128)S(1)}, u32[]{:S(2)}, u32[]{:S(2)}) %collective-permute-start.5) | collective-permute-done | bytes 163872 | tf_op jit(solution)/shard_map/ppermute | solution.py:236
  40.2 2.8 %collective-permute-start.6 = (f32[64,640]{1,0:T(8,128)S(1)}, f32[64,640]{1,0:T(8,128)S(1)}, u32[]{:S(2)}, u32[]{:S(2)}) collective-permute-start(f32[64,640]{1,0:T(8,128)S(1)} %add.82), channel_id=1, source_target_pairs={{0,16},{4,20},{8,24},{12,28},{16,0},{20,4},{24,8},{28,12},{1,17},{... | collective-permute-start | bytes 491528 | tf_op jit(solution)/shard_map/ppermute | solution.py:236
  43.1 5.2 %collective-permute-done.6 = f32[64,640]{1,0:T(8,128)S(1)} collective-permute-done((f32[64,640]{1,0:T(8,128)S(1)}, f32[64,640]{1,0:T(8,128)S(1)}, u32[]{:S(2)}, u32[]{:S(2)}) %collective-permute-start.6) | collective-permute-done | bytes 163872 | tf_op jit(solution)/shard_map/ppermute | solution.py:236
  48.3 1.6 collective-permute-start.7
  51.3 2.3 %collective-permute-done.7.other_ref = f32[64,640]{1,0:T(8,128)S(1)} collective-permute-done((f32[64,640]{1,0:T(8,128)S(1)}, f32[64,640]{1,0:T(8,128)S(1)}, u32[]{:S(2)}, u32[]{:S(2)}) %collective-permute-start.7) | collective-permute-done | bytes 163872 | tf_op jit(solution)/shard_map/ppermute | solution.py:236
  56.8 3.3 %collective-permute-done.9 = f32[72,64]{1,0:T(8,128)S(1)} collective-permute-done((f32[72,64]{1,0:T(8,128)S(1)}, f32[72,64]{1,0:T(8,128)S(1)}, u32[]{:S(2)}, u32[]{:S(2)}) %collective-permute-start.9) | collective-permute-done | bytes 18464 | tf_op jit(solution)/shard_map/ppermute | solution.py:236
  60.1 1.6 collective-permute-start.10
  61.7 2.1 %collective-permute-done.10 = f32[8,64]{1,0:T(8,128)S(1)} collective-permute-done((f32[8,64]{1,0:T(8,128)S(1)}, f32[8,64]{1,0:T(8,128)S(1)}, u32[]{:S(2)}, u32[]{:S(2)}) %collective-permute-start.10) | collective-permute-done | bytes 2080 | tf_op jit(solution)/shard_map/ppermute | solution.py:236
  64.6 4.0 %shard_map.67.refs_1_ = f32[6,64,1024]{2,1,0:T(8,128)S(1)} custom-call(f32[64,1024]{1,0:T(8,128)S(1)} %get-tuple-element.68.level_ref, bf16[8,1024,1024]{2,1,0:T(8,128)(2,1)S(1)} %get-tuple-element.56.tensor_ref), custom_call_target="tpu_custom_call" | custom-call | flops 805306368 | bytes 1000000 | tf_op jit(solution)/shard_map/pallas_call | solution.py:223
  68.6 3.4 %collective-permute-start.12 = (f32[8,64]{1,0:T(8,128)S(1)}, f32[8,64]{1,0:T(8,128)S(1)}, u32[]{:S(2)}, u32[]{:S(2)}) collective-permute-start(f32[8,64]{1,0:T(8,128)S(1)} %add.87.mine_ref), channel_id=1, source_target_pairs={{0,16},{4,20},{8,24},{12,28},{16,0},{20,4},{24,8},{28,12},{1,17},{... | collective-permute-start | bytes 6152 | tf_op jit(solution)/shard_map/ppermute | solution.py:236
  77.7 6.0 %shard_map.69 = (f32[64,64]{1,0:T(8,128)S(1)}, bf16[8,1024,1024]{2,1,0:T(8,128)(2,1)S(1)}) custom-call(f32[64,64]{1,0:T(8,128)S(1)} %get-tuple-element.69.system_ref, bf16[8,1024,1024]{2,1,0:T(8,128)(2,1)} %tensor_ref.7), custom_call_target="tpu_custom_call" | custom-call | flops 1073741824 | bytes 1000000 | tf_op jit(solution)/shard_map/pallas_call | solution.py:223
  83.7 1.8 collective-permute-done.14.other_ref
  85.4 4.1 %shard_map.70 = (f32[64,1024]{1,0:T(8,128)}, f32[8,64,1024]{2,1,0:T(8,128)S(1)}, f32[64,640]{1,0:T(8,128)S(1)}, f32[64,640]{1,0:T(8,128)S(1)}) custom-call(s32[1]{0:T(128)} %bitcast.side_ref, f32[64,64]{1,0:T(8,128)S(1)} %get-tuple-element.70.inverse_ref, f32[64,1024]{1,0:T(8,128)S(1)} %add.88.mine_ref, f32[64,1024]{1,0:T(8,128)S(1)} %collective-permute-done.14.other_ref, ...), custom_call_target="tpu_custom_call" | custom-call | flops 1073741824 | bytes 1000000 | tf_op jit(solution)/shard_map/pallas_call | solution.py:223
  89.5 1.5 collective-permute-start.15
  91.1 3.9 %collective-permute-done.15 = f32[64,640]{1,0:T(8,128)S(1)} collective-permute-done((f32[64,640]{1,0:T(8,128)S(1)}, f32[64,640]{1,0:T(8,128)S(1)}, u32[]{:S(2)}, u32[]{:S(2)}) %collective-permute-start.15) | collective-permute-done | bytes 163872 | tf_op jit(solution)/shard_map/ppermute | solution.py:236
  95.0 5.3 %collective-permute-done.16 = f32[64,640]{1,0:T(8,128)S(1)} collective-permute-done((f32[64,640]{1,0:T(8,128)S(1)}, f32[64,640]{1,0:T(8,128)S(1)}, u32[]{:S(2)}, u32[]{:S(2)}) %collective-permute-start.16) | collective-permute-done | bytes 163872 | tf_op jit(solution)/shard_map/ppermute | solution.py:236
  100.3 2.3 %collective-permute-start.17 = (f32[64,640]{1,0:T(8,128)S(1)}, f32[64,640]{1,0:T(8,128)S(1)}, u32[]{:S(2)}, u32[]{:S(2)}) collective-permute-start(f32[64,640]{1,0:T(8,128)S(1)} %add.90), channel_id=1, source_target_pairs={{0,16},{4,20},{8,24},{12,28},{16,0},{20,4},{24,8},{28,12},{1,17},{... | collective-permute-start | bytes 491528 | tf_op jit(solution)/shard_map/ppermute | solution.py:236
  102.6 5.5 %collective-permute-done.17 = f32[64,640]{1,0:T(8,128)S(1)} collective-permute-done((f32[64,640]{1,0:T(8,128)S(1)}, f32[64,640]{1,0:T(8,128)S(1)}, u32[]{:S(2)}, u32[]{:S(2)}) %collective-permute-start.17) | collective-permute-done | bytes 163872 | tf_op jit(solution)/shard_map/ppermute | solution.py:236
  108.1 1.6 collective-permute-start.18
  111.1 2.3 %collective-permute-done.18.other_ref = f32[64,640]{1,0:T(8,128)S(1)} collective-permute-done((f32[64,640]{1,0:T(8,128)S(1)}, f32[64,640]{1,0:T(8,128)S(1)}, u32[]{:S(2)}, u32[]{:S(2)}) %collective-permute-start.18) | collective-permute-done | bytes 163872 | tf_op jit(solution)/shard_map/ppermute | solution.py:236
  116.5 3.4 %collective-permute-done.20 = f32[72,64]{1,0:T(8,128)S(1)} collective-permute-done((f32[72,64]{1,0:T(8,128)S(1)}, f32[72,64]{1,0:T(8,128)S(1)}, u32[]{:S(2)}, u32[]{:S(2)}) %collective-permute-start.20) | collective-permute-done | bytes 18464 | tf_op jit(solution)/shard_map/ppermute | solution.py:236
  119.9 1.6 collective-permute-start.21
  121.5 2.1 %collective-permute-done.21 = f32[8,64]{1,0:T(8,128)S(1)} collective-permute-done((f32[8,64]{1,0:T(8,128)S(1)}, f32[8,64]{1,0:T(8,128)S(1)}, u32[]{:S(2)}, u32[]{:S(2)}) %collective-permute-start.21) | collective-permute-done | bytes 2080 | tf_op jit(solution)/shard_map/ppermute | solution.py:236
  123.6 4.1 %shard_map.75.refs_1_ = f32[6,64,1024]{2,1,0:T(8,128)S(1)} custom-call(f32[64,1024]{1,0:T(8,128)S(1)} %get-tuple-element.85.level_ref, bf16[8,1024,1024]{2,1,0:T(8,128)(2,1)S(1)} %get-tuple-element.73.tensor_ref), custom_call_target="tpu_custom_call" | custom-call | flops 805306368 | bytes 1000000 | tf_op jit(solution)/shard_map/pallas_call | solution.py:223
  135.0 6.0 %shard_map.77 = (f32[64,64]{1,0:T(8,128)S(1)}, bf16[8,1024,1024]{2,1,0:T(8,128)(2,1)S(1)}) custom-call(f32[64,64]{1,0:T(8,128)S(1)} %get-tuple-element.86.system_ref, bf16[8,1024,1024]{2,1,0:T(8,128)(2,1)} %tensor_ref.7), custom_call_target="tpu_custom_call" | custom-call | flops 1073741824 | bytes 1000000 | tf_op jit(solution)/shard_map/pallas_call | solution.py:223
  141.0 1.8 collective-permute-done.25.other_ref
  142.8 3.6 %shard_map.78 = (f32[64,1024]{1,0:T(8,128)S(1)}, f32[8,64,1024]{2,1,0:T(8,128)S(1)}, f32[64,640]{1,0:T(8,128)S(1)}, f32[64,640]{1,0:T(8,128)S(1)}) custom-call(s32[1]{0:T(128)} %bitcast.side_ref, f32[64,64]{1,0:T(8,128)S(1)} %get-tuple-element.87.inverse_ref, f32[64,1024]{1,0:T(8,128)S(1)} %add.96.mine_ref, ...), custom_call_target="tpu_custom_call" | custom-call | flops 1073741824 | bytes 1000000 | tf_op jit(solution)/shard_map/pallas_call | solution.py:223
  146.3 1.6 collective-permute-start.26
  147.9 3.9 %collective-permute-done.26 = f32[64,640]{1,0:T(8,128)S(1)} collective-permute-done((f32[64,640]{1,0:T(8,128)S(1)}, f32[64,640]{1,0:T(8,128)S(1)}, u32[]{:S(2)}, u32[]{:S(2)}) %collective-permute-start.26) | collective-permute-done | bytes 163872 | tf_op jit(solution)/shard_map/ppermute | solution.py:236
  151.8 2.1 %collective-permute-start.27 = (f32[64,640]{1,0:T(8,128)S(1)}, f32[64,640]{1,0:T(8,128)S(1)}, u32[]{:S(2)}, u32[]{:S(2)}) collective-permute-start(f32[64,640]{1,0:T(8,128)S(1)} %add.97), channel_id=1, source_target_pairs={{0,8},{4,12},{8,0},{12,4},{16,24},{20,28},{24,16},{28,20},{1,9},{5... | collective-permute-start | bytes 491528 | tf_op jit(solution)/shard_map/ppermute | solution.py:236
  153.9 3.3 %collective-permute-done.27 = f32[64,640]{1,0:T(8,128)S(1)} collective-permute-done((f32[64,640]{1,0:T(8,128)S(1)}, f32[64,640]{1,0:T(8,128)S(1)}, u32[]{:S(2)}, u32[]{:S(2)}) %collective-permute-start.27) | collective-permute-done | bytes 163872 | tf_op jit(solution)/shard_map/ppermute | solution.py:236
  158.5 5.0 %collective-permute-done.28 = f32[64,640]{1,0:T(8,128)S(1)} collective-permute-done((f32[64,640]{1,0:T(8,128)S(1)}, f32[64,640]{1,0:T(8,128)S(1)}, u32[]{:S(2)}, u32[]{:S(2)}) %collective-permute-start.28) | collective-permute-done | bytes 163872 | tf_op jit(solution)/shard_map/ppermute | solution.py:236
  163.6 1.6 collective-permute-start.29
  166.6 2.3 %collective-permute-done.29.other_ref = f32[64,640]{1,0:T(8,128)S(1)} collective-permute-done((f32[64,640]{1,0:T(8,128)S(1)}, f32[64,640]{1,0:T(8,128)S(1)}, u32[]{:S(2)}, u32[]{:S(2)}) %collective-permute-start.29) | collective-permute-done | bytes 163872 | tf_op jit(solution)/shard_map/ppermute | solution.py:236
  172.0 3.4 %collective-permute-done.31 = f32[72,64]{1,0:T(8,128)S(1)} collective-permute-done((f32[72,64]{1,0:T(8,128)S(1)}, f32[72,64]{1,0:T(8,128)S(1)}, u32[]{:S(2)}, u32[]{:S(2)}) %collective-permute-start.31) | collective-permute-done | bytes 18464 | tf_op jit(solution)/shard_map/ppermute | solution.py:236
  175.4 1.6 collective-permute-start.32
  179.3 2.5 %collective-permute-start.33 = (f32[8,64]{1,0:T(8,128)S(1)}, f32[8,64]{1,0:T(8,128)S(1)}, u32[]{:S(2)}, u32[]{:S(2)}) collective-permute-start(f32[8,64]{1,0:T(8,128)S(1)} %slice_add_fusion), channel_id=1, source_target_pairs={{0,8},{4,12},{8,0},{12,4},{16,24},{20,28},{24,16},{28,20},{1,9},{5... | collective-permute-start | bytes 6152 | tf_op jit(solution)/shard_map/ppermute | solution.py:236
  181.8 1.6 collective-permute-done.33
  183.4 2.2 %collective-permute-start.34 = (f32[8,64]{1,0:T(8,128)S(1)}, f32[8,64]{1,0:T(8,128)S(1)}, u32[]{:S(2)}, u32[]{:S(2)}) collective-permute-start(f32[8,64]{1,0:T(8,128)S(1)} %add.103.mine_ref), channel_id=1, source_target_pairs={{0,16},{4,20},{8,24},{12,28},{16,0},{20,4},{24,8},{28,12},{1,17},{... | collective-permute-start | bytes 6152 | tf_op jit(solution)/shard_map/ppermute | solution.py:236
  186.3 1.5 collective-permute-done.34.other_ref
  (88 shorter events, 38.3 us)
Async XLA Ops:
  0.6 1.0 copy-start
  1.9 1.4 collective-permute-start
  3.4 11.6 %collective-permute-start.1 = (f32[64,64]{1,0:T(8,128)S(1)}, f32[64,64]{1,0:T(8,128)S(1)}, u32[]{:S(2)}, u32[]{:S(2)}) collective-permute-start(f32[64,64]{1,0:T(8,128)S(1)} %add.78), channel_id=1, source_target_pairs={{0,2},{1,3},{2,0},{3,1},{4,6},{5,7},{6,4},{7,5},{8,10},{9,11},{10,... | collective-permute-start | bytes 49160 | tf_op jit(solution)/shard_map/ppermute | solution.py:236
  6.2 0.9 copy-start.1
  7.1 7.7 %copy-start.2 = (f32[8,64]{1,0:T(8,128)S(1)}, f32[8,64]{1,0:T(8,128)}, u32[]{:S(2)}) copy-start(f32[8,64]{1,0:T(8,128)} %time_ref.1) | copy-start | bytes 6148
  15.3 1.6 collective-permute-start.2
  16.9 8.4 %collective-permute-start.3 = (f32[64,1024]{1,0:T(8,128)S(1)}, f32[64,1024]{1,0:T(8,128)S(1)}, u32[]{:S(2)}, u32[]{:S(2)}) collective-permute-start(f32[64,1024]{1,0:T(8,128)S(1)} %add.80.mine_ref), channel_id=1, source_target_pairs={{0,2},{1,3},{2,0},{3,1},{4,6},{5,7},{6,4},{7,5},{8,10},{9,11},{10,... | collective-permute-start | bytes 786440 | tf_op jit(solution)/shard_map/ppermute | solution.py:236
  29.4 5.4 %collective-permute-start.4 = (f32[64,640]{1,0:T(8,128)S(1)}, f32[64,640]{1,0:T(8,128)S(1)}, u32[]{:S(2)}, u32[]{:S(2)}) collective-permute-start(f32[64,640]{1,0:T(8,128)S(1)} %get-tuple-element.58), channel_id=1, source_target_pairs={{0,4},{4,0},{8,12},{12,8},{16,20},{20,16},{24,28},{28,24},{1,5},{5... | collective-permute-start | bytes 491528 | tf_op jit(solution)/shard_map/ppermute | solution.py:236
  34.8 5.4 %collective-permute-start.5 = (f32[64,640]{1,0:T(8,128)S(1)}, f32[64,640]{1,0:T(8,128)S(1)}, u32[]{:S(2)}, u32[]{:S(2)}) collective-permute-start(f32[64,640]{1,0:T(8,128)S(1)} %add.81), channel_id=1, source_target_pairs={{0,8},{4,12},{8,0},{12,4},{16,24},{20,28},{24,16},{28,20},{1,9},{5... | collective-permute-start | bytes 491528 | tf_op jit(solution)/shard_map/ppermute | solution.py:236
  40.2 8.0 %collective-permute-start.6 = (f32[64,640]{1,0:T(8,128)S(1)}, f32[64,640]{1,0:T(8,128)S(1)}, u32[]{:S(2)}, u32[]{:S(2)}) collective-permute-start(f32[64,640]{1,0:T(8,128)S(1)} %add.82), channel_id=1, source_target_pairs={{0,16},{4,20},{8,24},{12,28},{16,0},{20,4},{24,8},{28,12},{1,17},{... | collective-permute-start | bytes 491528 | tf_op jit(solution)/shard_map/ppermute | solution.py:236
  48.3 5.4 %collective-permute-start.7 = (f32[64,640]{1,0:T(8,128)S(1)}, f32[64,640]{1,0:T(8,128)S(1)}, u32[]{:S(2)}, u32[]{:S(2)}) collective-permute-start(f32[64,640]{1,0:T(8,128)S(1)} %add.83.mine_ref), channel_id=1, source_target_pairs={{0,4},{4,0},{8,12},{12,8},{16,20},{20,16},{24,28},{28,24},{1,5},{5... | collective-permute-start | bytes 491528 | tf_op jit(solution)/shard_map/ppermute | solution.py:236
  54.9 1.3 collective-permute-start.8
  56.1 4.0 %collective-permute-start.9 = (f32[72,64]{1,0:T(8,128)S(1)}, f32[72,64]{1,0:T(8,128)S(1)}, u32[]{:S(2)}, u32[]{:S(2)}) collective-permute-start(f32[72,64]{1,0:T(8,128)S(1)} %add.84), channel_id=1, source_target_pairs={{0,2},{1,3},{2,0},{3,1},{4,6},{5,7},{6,4},{7,5},{8,10},{9,11},{10,... | collective-permute-start | bytes 55304 | tf_op jit(solution)/shard_map/ppermute | solution.py:236
  60.1 3.7 %collective-permute-start.10 = (f32[8,64]{1,0:T(8,128)S(1)}, f32[8,64]{1,0:T(8,128)S(1)}, u32[]{:S(2)}, u32[]{:S(2)}) collective-permute-start(f32[8,64]{1,0:T(8,128)S(1)} %slice.16), channel_id=1, source_target_pairs={{0,4},{4,0},{8,12},{12,8},{16,20},{20,16},{24,28},{28,24},{1,5},{5... | collective-permute-start | bytes 6152 | tf_op jit(solution)/shard_map/ppermute | solution.py:236
  63.8 4.8 %collective-permute-start.11 = (f32[8,64]{1,0:T(8,128)S(1)}, f32[8,64]{1,0:T(8,128)S(1)}, u32[]{:S(2)}, u32[]{:S(2)}) collective-permute-start(f32[8,64]{1,0:T(8,128)S(1)} %slice_add_fusion.2), channel_id=1, source_target_pairs={{0,8},{4,12},{8,0},{12,4},{16,24},{20,28},{24,16},{28,20},{1,9},{5... | collective-permute-start | bytes 6152 | tf_op jit(solution)/shard_map/ppermute | solution.py:236
  68.6 6.3 %collective-permute-start.12 = (f32[8,64]{1,0:T(8,128)S(1)}, f32[8,64]{1,0:T(8,128)S(1)}, u32[]{:S(2)}, u32[]{:S(2)}) collective-permute-start(f32[8,64]{1,0:T(8,128)S(1)} %add.87.mine_ref), channel_id=1, source_target_pairs={{0,16},{4,20},{8,24},{12,28},{16,0},{20,4},{24,8},{28,12},{1,17},{... | collective-permute-start | bytes 6152 | tf_op jit(solution)/shard_map/ppermute | solution.py:236
  75.4 1.6 collective-permute-start.13
  77.0 8.4 %collective-permute-start.14 = (f32[64,1024]{1,0:T(8,128)S(1)}, f32[64,1024]{1,0:T(8,128)S(1)}, u32[]{:S(2)}, u32[]{:S(2)}) collective-permute-start(f32[64,1024]{1,0:T(8,128)S(1)} %add.88.mine_ref), channel_id=1, source_target_pairs={{0,2},{1,3},{2,0},{3,1},{4,6},{5,7},{6,4},{7,5},{8,10},{9,11},{10,... | collective-permute-start | bytes 786440 | tf_op jit(solution)/shard_map/ppermute | solution.py:236
  89.5 5.4 %collective-permute-start.15 = (f32[64,640]{1,0:T(8,128)S(1)}, f32[64,640]{1,0:T(8,128)S(1)}, u32[]{:S(2)}, u32[]{:S(2)}) collective-permute-start(f32[64,640]{1,0:T(8,128)S(1)} %get-tuple-element.75), channel_id=1, source_target_pairs={{0,4},{4,0},{8,12},{12,8},{16,20},{20,16},{24,28},{28,24},{1,5},{5... | collective-permute-start | bytes 491528 | tf_op jit(solution)/shard_map/ppermute | solution.py:236
  94.9 5.4 %collective-permute-start.16 = (f32[64,640]{1,0:T(8,128)S(1)}, f32[64,640]{1,0:T(8,128)S(1)}, u32[]{:S(2)}, u32[]{:S(2)}) collective-permute-start(f32[64,640]{1,0:T(8,128)S(1)} %add.89), channel_id=1, source_target_pairs={{0,8},{4,12},{8,0},{12,4},{16,24},{20,28},{24,16},{28,20},{1,9},{5... | collective-permute-start | bytes 491528 | tf_op jit(solution)/shard_map/ppermute | solution.py:236
  100.3 7.7 %collective-permute-start.17 = (f32[64,640]{1,0:T(8,128)S(1)}, f32[64,640]{1,0:T(8,128)S(1)}, u32[]{:S(2)}, u32[]{:S(2)}) collective-permute-start(f32[64,640]{1,0:T(8,128)S(1)} %add.90), channel_id=1, source_target_pairs={{0,16},{4,20},{8,24},{12,28},{16,0},{20,4},{24,8},{28,12},{1,17},{... | collective-permute-start | bytes 491528 | tf_op jit(solution)/shard_map/ppermute | solution.py:236
  108.1 5.4 %collective-permute-start.18 = (f32[64,640]{1,0:T(8,128)S(1)}, f32[64,640]{1,0:T(8,128)S(1)}, u32[]{:S(2)}, u32[]{:S(2)}) collective-permute-start(f32[64,640]{1,0:T(8,128)S(1)} %add.91.mine_ref), channel_id=1, source_target_pairs={{0,4},{4,0},{8,12},{12,8},{16,20},{20,16},{24,28},{28,24},{1,5},{5... | collective-permute-start | bytes 491528 | tf_op jit(solution)/shard_map/ppermute | solution.py:236
  114.6 1.3 collective-permute-start.19
  115.9 4.0 %collective-permute-start.20 = (f32[72,64]{1,0:T(8,128)S(1)}, f32[72,64]{1,0:T(8,128)S(1)}, u32[]{:S(2)}, u32[]{:S(2)}) collective-permute-start(f32[72,64]{1,0:T(8,128)S(1)} %add.92), channel_id=1, source_target_pairs={{0,2},{1,3},{2,0},{3,1},{4,6},{5,7},{6,4},{7,5},{8,10},{9,11},{10,... | collective-permute-start | bytes 55304 | tf_op jit(solution)/shard_map/ppermute | solution.py:236
  119.9 3.7 %collective-permute-start.21 = (f32[8,64]{1,0:T(8,128)S(1)}, f32[8,64]{1,0:T(8,128)S(1)}, u32[]{:S(2)}, u32[]{:S(2)}) collective-permute-start(f32[8,64]{1,0:T(8,128)S(1)} %slice.17), channel_id=1, source_target_pairs={{0,4},{4,0},{8,12},{12,8},{16,20},{20,16},{24,28},{28,24},{1,5},{5... | collective-permute-start | bytes 6152 | tf_op jit(solution)/shard_map/ppermute | solution.py:236
  123.6 4.1 %collective-permute-start.22 = (f32[8,64]{1,0:T(8,128)S(1)}, f32[8,64]{1,0:T(8,128)S(1)}, u32[]{:S(2)}, u32[]{:S(2)}) collective-permute-start(f32[8,64]{1,0:T(8,128)S(1)} %slice_add_fusion.1), channel_id=1, source_target_pairs={{0,8},{4,12},{8,0},{12,4},{16,24},{20,28},{24,16},{28,20},{1,9},{5... | collective-permute-start | bytes 6152 | tf_op jit(solution)/shard_map/ppermute | solution.py:236
  127.7 4.6 %collective-permute-start.23 = (f32[8,64]{1,0:T(8,128)S(1)}, f32[8,64]{1,0:T(8,128)S(1)}, u32[]{:S(2)}, u32[]{:S(2)}) collective-permute-start(f32[8,64]{1,0:T(8,128)S(1)} %add.95.mine_ref), channel_id=1, source_target_pairs={{0,16},{4,20},{8,24},{12,28},{16,0},{20,4},{24,8},{28,12},{1,17},{... | collective-permute-start | bytes 6152 | tf_op jit(solution)/shard_map/ppermute | solution.py:236
  132.7 1.6 collective-permute-start.24
  134.4 8.4 %collective-permute-start.25 = (f32[64,1024]{1,0:T(8,128)S(1)}, f32[64,1024]{1,0:T(8,128)S(1)}, u32[]{:S(2)}, u32[]{:S(2)}) collective-permute-start(f32[64,1024]{1,0:T(8,128)S(1)} %add.96.mine_ref), channel_id=1, source_target_pairs={{0,2},{1,3},{2,0},{3,1},{4,6},{5,7},{6,4},{7,5},{8,10},{9,11},{10,... | collective-permute-start | bytes 786440 | tf_op jit(solution)/shard_map/ppermute | solution.py:236
  146.3 5.5 %collective-permute-start.26 = (f32[64,640]{1,0:T(8,128)S(1)}, f32[64,640]{1,0:T(8,128)S(1)}, u32[]{:S(2)}, u32[]{:S(2)}) collective-permute-start(f32[64,640]{1,0:T(8,128)S(1)} %get-tuple-element.93), channel_id=1, source_target_pairs={{0,4},{4,0},{8,12},{12,8},{16,20},{20,16},{24,28},{28,24},{1,5},{5... | collective-permute-start | bytes 491528 | tf_op jit(solution)/shard_map/ppermute | solution.py:236
  151.8 5.4 %collective-permute-start.27 = (f32[64,640]{1,0:T(8,128)S(1)}, f32[64,640]{1,0:T(8,128)S(1)}, u32[]{:S(2)}, u32[]{:S(2)}) collective-permute-start(f32[64,640]{1,0:T(8,128)S(1)} %add.97), channel_id=1, source_target_pairs={{0,8},{4,12},{8,0},{12,4},{16,24},{20,28},{24,16},{28,20},{1,9},{5... | collective-permute-start | bytes 491528 | tf_op jit(solution)/shard_map/ppermute | solution.py:236
  157.3 6.3 %collective-permute-start.28 = (f32[64,640]{1,0:T(8,128)S(1)}, f32[64,640]{1,0:T(8,128)S(1)}, u32[]{:S(2)}, u32[]{:S(2)}) collective-permute-start(f32[64,640]{1,0:T(8,128)S(1)} %add.98), channel_id=1, source_target_pairs={{0,16},{4,20},{8,24},{12,28},{16,0},{20,4},{24,8},{28,12},{1,17},{... | collective-permute-start | bytes 491528 | tf_op jit(solution)/shard_map/ppermute | solution.py:236
  163.6 5.4 %collective-permute-start.29 = (f32[64,640]{1,0:T(8,128)S(1)}, f32[64,640]{1,0:T(8,128)S(1)}, u32[]{:S(2)}, u32[]{:S(2)}) collective-permute-start(f32[64,640]{1,0:T(8,128)S(1)} %add.99.mine_ref), channel_id=1, source_target_pairs={{0,4},{4,0},{8,12},{12,8},{16,20},{20,16},{24,28},{28,24},{1,5},{5... | collective-permute-start | bytes 491528 | tf_op jit(solution)/shard_map/ppermute | solution.py:236
  170.2 1.3 collective-permute-start.30
  171.4 4.0 %collective-permute-start.31 = (f32[72,64]{1,0:T(8,128)S(1)}, f32[72,64]{1,0:T(8,128)S(1)}, u32[]{:S(2)}, u32[]{:S(2)}) collective-permute-start(f32[72,64]{1,0:T(8,128)S(1)} %add.100), channel_id=1, source_target_pairs={{0,2},{1,3},{2,0},{3,1},{4,6},{5,7},{6,4},{7,5},{8,10},{9,11},{10,... | collective-permute-start | bytes 55304 | tf_op jit(solution)/shard_map/ppermute | solution.py:236
  175.4 3.8 %collective-permute-start.32 = (f32[8,64]{1,0:T(8,128)S(1)}, f32[8,64]{1,0:T(8,128)S(1)}, u32[]{:S(2)}, u32[]{:S(2)}) collective-permute-start(f32[8,64]{1,0:T(8,128)S(1)} %slice.18), channel_id=1, source_target_pairs={{0,4},{4,0},{8,12},{12,8},{16,20},{20,16},{24,28},{28,24},{1,5},{5... | collective-permute-start | bytes 6152 | tf_op jit(solution)/shard_map/ppermute | solution.py:236
  179.3 4.1 %collective-permute-start.33 = (f32[8,64]{1,0:T(8,128)S(1)}, f32[8,64]{1,0:T(8,128)S(1)}, u32[]{:S(2)}, u32[]{:S(2)}) collective-permute-start(f32[8,64]{1,0:T(8,128)S(1)} %slice_add_fusion), channel_id=1, source_target_pairs={{0,8},{4,12},{8,0},{12,4},{16,24},{20,28},{24,16},{28,20},{1,9},{5... | collective-permute-start | bytes 6152 | tf_op jit(solution)/shard_map/ppermute | solution.py:236
  183.4 4.5 %collective-permute-start.34 = (f32[8,64]{1,0:T(8,128)S(1)}, f32[8,64]{1,0:T(8,128)S(1)}, u32[]{:S(2)}, u32[]{:S(2)}) collective-permute-start(f32[8,64]{1,0:T(8,128)S(1)} %add.103.mine_ref), channel_id=1, source_target_pairs={{0,16},{4,20},{8,24},{12,28},{16,0},{20,4},{24,8},{28,12},{1,17},{... | collective-permute-start | bytes 6152 | tf_op jit(solution)/shard_map/ppermute | solution.py:236

commit v3 on v2

--- a/solution.py
+++ b/solution.py
@@ -14,7 +14,7 @@
 HIGHEST = lax.Precision.HIGHEST
 F32 = jnp.float32
 LOOK = 4
-PIECES = (2, 6)
+PIECES = (1, 2, 5)
 
 
 def exact_dot(a, b, dims=(((1,), (0,)), ((), ()))):
@@ -159,14 +159,15 @@
 def level_pass_kernel(
     side_ref, inverse_ref, mine_ref, other_ref, time_cols_ref, tensor_ref, solved_ref, parts_ref, keep_ref, send_ref, sums
 ):
+    n = inverse_ref.shape[0]
     half = sums.shape[2]
     solved = exact_dot(inverse_ref[...], mine_ref[...] + other_ref[...])
     solved_ref[...] = solved
     rounded = solved.astype(jnp.bfloat16)
     gram = exact_dot(solved, solved, NT)
-    gram = jnp.concatenate([gram, jnp.zeros_like(gram)], axis=1)
-    keep_ref[:, half:] = gram
-    send_ref[:, half:] = gram
+    packed = jnp.concatenate([gram[8 * b : 8 * b + 8] for b in range(n // 8)], axis=1)
+    keep_ref[n:] = packed
+    send_ref[n:] = packed
     for k in range(tensor_ref.shape[0]):
         product = jnp.dot(rounded, tensor_ref[k], preferred_element_type=F32)
         parts_ref[k] = product
@@ -175,14 +176,13 @@
             piece = weighted[:, i * half : (i + 1) * half]
             sums[i] = piece if k == 0 else sums[i] + piece
     side = side_ref[0]
-    keep_ref[:, :half] = sums[side]
-    send_ref[:, :half] = sums[1 - side]
+    keep_ref[:n] = sums[side]
+    send_ref[:n] = sums[1 - side]
 
 
 def level_weights_kernel(mine_ref, tgram_ref, weights_ref, pgram_ref, pscale_ref, *, count):
     n = tgram_ref.shape[0]
-    half = mine_ref.shape[1] - 2 * n
-    raw = mine_ref[:, half : half + n]
+    raw = jnp.concatenate([mine_ref[n:, n * b : n * b + n] for b in range(n // 8)], axis=0)
     row, col = unit_scales(raw, count)
     pgram = col * raw * row
     pgram_ref[...] = pgram
@@ -195,8 +195,8 @@
     half = solved_ref.shape[1] // 2
     side = side_ref[0]
     weights = weights_ref[...]
-    solved_ref[:, pl.ds(pl.multiple_of(side * half, half), half)] = exact_dot(weights, mine_ref[:, :half])
-    solved_ref[:, pl.ds(pl.multiple_of((1 - side) * half, half), half)] = exact_dot(weights, other_ref[:, :half])
+    solved_ref[:, pl.ds(pl.multiple_of(side * half, half), half)] = exact_dot(weights, mine_ref[:n])
+    solved_ref[:, pl.ds(pl.multiple_of((1 - side) * half, half), half)] = exact_dot(weights, other_ref[:n])
     solved = solved_ref[...]
     small_ref[0:n] = exact_dot(solved, solved, NT)
     for k in range(parts_ref.shape[0]):
@@ -278,7 +278,7 @@
         held = pltpu.with_memory_space_constraint(held, V)
         point_solved, parts, keep, send = call(
             level_pass_kernel,
-            [shape(rank, points), shape(steps, rank, levels)] + [shape(rank, half + 2 * rank)] * 2,
+            [shape(rank, points), shape(steps, rank, levels)] + [shape(rank + 8, half)] * 2,
             side, inverse, mine, other, time.T, held,
             flops=flops, limit=24, spaces=[S] + [V] * 5,
             scratch=[V((2, rank, half), F32)],

time: 189 us -> 186 us (0.984)
  starting transfers between devices: 40.9 us -> 34.7 us
  waiting for transfers between devices: 80 us -> 82.7 us
    ppermute x35, starting transfers between devices: 40.9 us -> 34.7 us  [swap(): return lax.ppermute(x, axis, [(i, i ^ mask) for i in range(n)])]
    ppermute x35, waiting for transfers between devices: 80 us -> 82.7 us  [swap(): return lax.ppermute(x, axis, [(i, i ^ mask) for i in range(n)])]
    pallas_call x25 -> x27, Pallas kernels: 62.7 us -> 63.1 us  [call(): pl.pallas_call(kernel, out_shape=outs, in_specs=[pl.BlockSpec(memory_spac...]
  transfers between devices with their start and end apart: 35 -> 35, of which waited for: 30 -> 31; matrix products, arithmetic and copies ran while one was open for 1% -> 1% of each run, Pallas kernels for 24% -> 25%
where the time goes in v3:
time: 186 us
  waiting for transfers between devices  82.7 us (44%)
  Pallas kernels  63.1 us (34%)
  starting transfers between devices  34.7 us (19%)
  local copies, waits for them, and re-layouts  2.17 us (1%)
  other arithmetic  1.93 us (1%)
    ppermute x35, waiting for transfers between devices, swap(): return lax.ppermute(x, axis, [(i, i ^ mask) for i in range(n)])  82.7 us
    pallas_call x27, Pallas kernels, call(): pl.pallas_call(kernel, out_shape=outs, in_specs=[pl.BlockSpec(memory_spac...  63.1 us
    ppermute x35, starting transfers between devices, swap(): return lax.ppermute(x, axis, [(i, i ^ mask) for i in range(n)])  34.7 us
  transfers between devices with their start and end apart: 35, of which 31 were waited for; matrix products, arithmetic and copies ran while one was open for 1% of the time, Pallas kernels for 25%

profile of v3, /device:TPU:0, one launch (start us, length us, event | category | flops | bytes accessed | tf_op | source)
XLA Modules:
  0.0 185.5 jit_solution(7842339089731144518)
XLA Ops:
  3.4 2.8 %collective-permute-start.1 = (f32[64,64]{1,0:T(8,128)S(1)}, f32[64,64]{1,0:T(8,128)S(1)}, u32[]{:S(2)}, u32[]{:S(2)}) collective-permute-start(f32[64,64]{1,0:T(8,128)S(1)} %add.78), channel_id=1, source_target_pairs={{0,2},{1,3},{2,0},{3,1},{4,6},{5,7},{6,4},{7,5},{8,10},{9,11},{10,... | collective-permute-start | bytes 49160 | tf_op jit(solution)/shard_map/ppermute | solution.py:236
  7.1 7.7 %shard_map.59.refs_0_ = f32[8,64,1024]{2,1,0:T(8,128)S(1)} custom-call(f32[64,1024]{1,0:T(8,128)S(1)} %copy-done.1, bf16[8,1024,1024]{2,1,0:T(8,128)(2,1)} %tensor_ref.7), custom_call_target="tpu_custom_call" | custom-call | flops 1073741824 | bytes 1000000 | tf_op jit(solution)/shard_map/pallas_call | solution.py:223
  15.3 1.5 collective-permute-done.2
  17.0 6.0 %shard_map.61 = (f32[64,64]{1,0:T(8,128)S(1)}, bf16[8,1024,1024]{2,1,0:T(8,128)(2,1)S(1)}) custom-call(f32[64,64]{1,0:T(8,128)S(1)} %get-tuple-element.53.system_ref, bf16[8,1024,1024]{2,1,0:T(8,128)(2,1)} %tensor_ref.7), custom_call_target="tpu_custom_call" | custom-call | flops 1073741824 | bytes 1000000 | tf_op jit(solution)/shard_map/pallas_call | solution.py:223
  23.0 2.4 %collective-permute-done.3.other_ref = f32[64,1024]{1,0:T(8,128)S(1)} collective-permute-done((f32[64,1024]{1,0:T(8,128)S(1)}, f32[64,1024]{1,0:T(8,128)S(1)}, u32[]{:S(2)}, u32[]{:S(2)}) %collective-permute-start.3) | collective-permute-done | bytes 262176 | tf_op jit(solution)/shard_map/ppermute | solution.py:236
  25.3 4.1 %shard_map.62 = (f32[64,1024]{1,0:T(8,128)}, f32[8,64,1024]{2,1,0:T(8,128)S(1)}, f32[72,512]{1,0:T(8,128)S(1)}, f32[72,512]{1,0:T(8,128)S(1)}) custom-call(s32[1]{0:T(128)} %bitcast.side_ref, f32[64,64]{1,0:T(8,128)S(1)} %get-tuple-element.54.inverse_ref, f32[64,1024]{1,0:T(8,128)S(1)} %add.80.mine_ref, f32[64,1024]{1,0:T(8,128)S(1)} %collective-permute-done.3.other_ref, ...), custom_call_target="tpu_custom_call" | custom-call | flops 1073741824 | bytes 1000000 | tf_op jit(solution)/shard_map/pallas_call | solution.py:223
  29.4 1.5 collective-permute-start.4
  30.9 3.6 %collective-permute-done.4 = f32[72,512]{1,0:T(8,128)S(1)} collective-permute-done((f32[72,512]{1,0:T(8,128)S(1)}, f32[72,512]{1,0:T(8,128)S(1)}, u32[]{:S(2)}, u32[]{:S(2)}) %collective-permute-start.4) | collective-permute-done | bytes 147488 | tf_op jit(solution)/shard_map/ppermute | solution.py:236
  34.6 1.6 collective-permute-start.5
  36.2 3.6 %collective-permute-done.5 = f32[72,512]{1,0:T(8,128)S(1)} collective-permute-done((f32[72,512]{1,0:T(8,128)S(1)}, f32[72,512]{1,0:T(8,128)S(1)}, u32[]{:S(2)}, u32[]{:S(2)}) %collective-permute-start.5) | collective-permute-done | bytes 147488 | tf_op jit(solution)/shard_map/ppermute | solution.py:236
  39.8 3.1 %collective-permute-start.6 = (f32[72,512]{1,0:T(8,128)S(1)}, f32[72,512]{1,0:T(8,128)S(1)}, u32[]{:S(2)}, u32[]{:S(2)}) collective-permute-start(f32[72,512]{1,0:T(8,128)S(1)} %add.82), channel_id=1, source_target_pairs={{0,16},{4,20},{8,24},{12,28},{16,0},{20,4},{24,8},{28,12},{1,17},{... | collective-permute-start | bytes 442376 | tf_op jit(solution)/shard_map/ppermute | solution.py:236
  42.9 4.7 %collective-permute-done.6 = f32[72,512]{1,0:T(8,128)S(1)} collective-permute-done((f32[72,512]{1,0:T(8,128)S(1)}, f32[72,512]{1,0:T(8,128)S(1)}, u32[]{:S(2)}, u32[]{:S(2)}) %collective-permute-start.6) | collective-permute-done | bytes 147488 | tf_op jit(solution)/shard_map/ppermute | solution.py:236
  47.7 1.6 collective-permute-start.7
  50.7 2.1 %collective-permute-done.7.other_ref = f32[72,512]{1,0:T(8,128)S(1)} collective-permute-done((f32[72,512]{1,0:T(8,128)S(1)}, f32[72,512]{1,0:T(8,128)S(1)}, u32[]{:S(2)}, u32[]{:S(2)}) %collective-permute-start.7) | collective-permute-done | bytes 147488 | tf_op jit(solution)/shard_map/ppermute | solution.py:236
  55.8 3.4 %collective-permute-done.9 = f32[72,64]{1,0:T(8,128)S(1)} collective-permute-done((f32[72,64]{1,0:T(8,128)S(1)}, f32[72,64]{1,0:T(8,128)S(1)}, u32[]{:S(2)}, u32[]{:S(2)}) %collective-permute-start.9) | collective-permute-done | bytes 18464 | tf_op jit(solution)/shard_map/ppermute | solution.py:236
  59.2 1.6 collective-permute-start.10
  60.8 3.4 %shard_map.68.refs_2_ = f32[5,64,1024]{2,1,0:T(8,128)S(1)} custom-call(f32[64,1024]{1,0:T(8,128)S(1)} %get-tuple-element.68.level_ref, bf16[8,1024,1024]{2,1,0:T(8,128)(2,1)S(1)} %get-tuple-element.56.tensor_ref), custom_call_target="tpu_custom_call" | custom-call | flops 671088640 | bytes 1000000 | tf_op jit(solution)/shard_map/pallas_call | solution.py:223
  66.4 1.6 collective-permute-done.11
  67.9 2.0 %collective-permute-start.12 = (f32[8,64]{1,0:T(8,128)S(1)}, f32[8,64]{1,0:T(8,128)S(1)}, u32[]{:S(2)}, u32[]{:S(2)}) collective-permute-start(f32[8,64]{1,0:T(8,128)S(1)} %add.87.mine_ref), channel_id=1, source_target_pairs={{0,16},{4,20},{8,24},{12,28},{16,0},{20,4},{24,8},{28,12},{1,17},{... | collective-permute-start | bytes 6152 | tf_op jit(solution)/shard_map/ppermute | solution.py:236
  73.0 1.5 collective-permute-done.13
  75.2 6.0 %shard_map.70 = (f32[64,64]{1,0:T(8,128)S(1)}, bf16[8,1024,1024]{2,1,0:T(8,128)(2,1)S(1)}) custom-call(f32[64,64]{1,0:T(8,128)S(1)} %get-tuple-element.69.system_ref, bf16[8,1024,1024]{2,1,0:T(8,128)(2,1)} %tensor_ref.7), custom_call_target="tpu_custom_call" | custom-call | flops 1073741824 | bytes 1000000 | tf_op jit(solution)/shard_map/pallas_call | solution.py:223
  81.2 1.8 collective-permute-done.14.other_ref
  83.0 4.1 %shard_map.71 = (f32[64,1024]{1,0:T(8,128)}, f32[8,64,1024]{2,1,0:T(8,128)S(1)}, f32[72,512]{1,0:T(8,128)S(1)}, f32[72,512]{1,0:T(8,128)S(1)}) custom-call(s32[1]{0:T(128)} %bitcast.side_ref, f32[64,64]{1,0:T(8,128)S(1)} %get-tuple-element.70.inverse_ref, f32[64,1024]{1,0:T(8,128)S(1)} %add.88.mine_ref, f32[64,1024]{1,0:T(8,128)S(1)} %collective-permute-done.14.other_ref, ...), custom_call_target="tpu_custom_call" | custom-call | flops 1073741824 | bytes 1000000 | tf_op jit(solution)/shard_map/pallas_call | solution.py:223
  87.6 4.6 %collective-permute-done.15 = f32[72,512]{1,0:T(8,128)S(1)} collective-permute-done((f32[72,512]{1,0:T(8,128)S(1)}, f32[72,512]{1,0:T(8,128)S(1)}, u32[]{:S(2)}, u32[]{:S(2)}) %collective-permute-start.15) | collective-permute-done | bytes 147488 | tf_op jit(solution)/shard_map/ppermute | solution.py:236
  92.2 1.8 collective-permute-start.16
  94.1 3.4 %collective-permute-done.16 = f32[72,512]{1,0:T(8,128)S(1)} collective-permute-done((f32[72,512]{1,0:T(8,128)S(1)}, f32[72,512]{1,0:T(8,128)S(1)}, u32[]{:S(2)}, u32[]{:S(2)}) %collective-permute-start.16) | collective-permute-done | bytes 147488 | tf_op jit(solution)/shard_map/ppermute | solution.py:236
  97.5 2.1 %collective-permute-start.17 = (f32[72,512]{1,0:T(8,128)S(1)}, f32[72,512]{1,0:T(8,128)S(1)}, u32[]{:S(2)}, u32[]{:S(2)}) collective-permute-start(f32[72,512]{1,0:T(8,128)S(1)} %add.90), channel_id=1, source_target_pairs={{0,16},{4,20},{8,24},{12,28},{16,0},{20,4},{24,8},{28,12},{1,17},{... | collective-permute-start | bytes 442376 | tf_op jit(solution)/shard_map/ppermute | solution.py:236
  99.6 5.6 %collective-permute-done.17 = f32[72,512]{1,0:T(8,128)S(1)} collective-permute-done((f32[72,512]{1,0:T(8,128)S(1)}, f32[72,512]{1,0:T(8,128)S(1)}, u32[]{:S(2)}, u32[]{:S(2)}) %collective-permute-start.17) | collective-permute-done | bytes 147488 | tf_op jit(solution)/shard_map/ppermute | solution.py:236
  107.3 3.1 %collective-permute-done.18.other_ref = f32[72,512]{1,0:T(8,128)S(1)} collective-permute-done((f32[72,512]{1,0:T(8,128)S(1)}, f32[72,512]{1,0:T(8,128)S(1)}, u32[]{:S(2)}, u32[]{:S(2)}) %collective-permute-start.18) | collective-permute-done | bytes 147488 | tf_op jit(solution)/shard_map/ppermute | solution.py:236
  113.4 3.4 %collective-permute-done.20 = f32[72,64]{1,0:T(8,128)S(1)} collective-permute-done((f32[72,64]{1,0:T(8,128)S(1)}, f32[72,64]{1,0:T(8,128)S(1)}, u32[]{:S(2)}, u32[]{:S(2)}) %collective-permute-start.20) | collective-permute-done | bytes 18464 | tf_op jit(solution)/shard_map/ppermute | solution.py:236
  117.4 3.3 %shard_map.77.refs_2_ = f32[5,64,1024]{2,1,0:T(8,128)S(1)} custom-call(f32[64,1024]{1,0:T(8,128)S(1)} %get-tuple-element.85.level_ref, bf16[8,1024,1024]{2,1,0:T(8,128)(2,1)S(1)} %get-tuple-element.73.tensor_ref), custom_call_target="tpu_custom_call" | custom-call | flops 671088640 | bytes 1000000 | tf_op jit(solution)/shard_map/pallas_call | solution.py:223
  121.0 1.5 shard_map.76.refs_1_
  122.5 1.8 collective-permute-done.22
  129.4 1.5 collective-permute-done.24
  131.6 6.0 %shard_map.79 = (f32[64,64]{1,0:T(8,128)S(1)}, bf16[8,1024,1024]{2,1,0:T(8,128)(2,1)S(1)}) custom-call(f32[64,64]{1,0:T(8,128)S(1)} %get-tuple-element.86.system_ref, bf16[8,1024,1024]{2,1,0:T(8,128)(2,1)} %tensor_ref.7), custom_call_target="tpu_custom_call" | custom-call | flops 1073741824 | bytes 1000000 | tf_op jit(solution)/shard_map/pallas_call | solution.py:223
  137.6 1.8 collective-permute-done.25.other_ref
  139.4 3.6 %shard_map.80 = (f32[64,1024]{1,0:T(8,128)S(1)}, f32[8,64,1024]{2,1,0:T(8,128)S(1)}, f32[72,512]{1,0:T(8,128)S(1)}, f32[72,512]{1,0:T(8,128)S(1)}) custom-call(s32[1]{0:T(128)} %bitcast.side_ref, f32[64,64]{1,0:T(8,128)S(1)} %get-tuple-element.87.inverse_ref, f32[64,1024]{1,0:T(8,128)S(1)} %add.96.mine_ref, ...), custom_call_target="tpu_custom_call" | custom-call | flops 1073741824 | bytes 1000000 | tf_op jit(solution)/shard_map/pallas_call | solution.py:223
  142.9 1.6 collective-permute-start.26
  144.5 3.6 %collective-permute-done.26 = f32[72,512]{1,0:T(8,128)S(1)} collective-permute-done((f32[72,512]{1,0:T(8,128)S(1)}, f32[72,512]{1,0:T(8,128)S(1)}, u32[]{:S(2)}, u32[]{:S(2)}) %collective-permute-start.26) | collective-permute-done | bytes 147488 | tf_op jit(solution)/shard_map/ppermute | solution.py:236
  149.4 4.0 %collective-permute-done.27 = f32[72,512]{1,0:T(8,128)S(1)} collective-permute-done((f32[72,512]{1,0:T(8,128)S(1)}, f32[72,512]{1,0:T(8,128)S(1)}, u32[]{:S(2)}, u32[]{:S(2)}) %collective-permute-start.27) | collective-permute-done | bytes 147488 | tf_op jit(solution)/shard_map/ppermute | solution.py:236
  153.4 1.5 collective-permute-start.28
  154.9 6.2 %collective-permute-done.28 = f32[72,512]{1,0:T(8,128)S(1)} collective-permute-done((f32[72,512]{1,0:T(8,128)S(1)}, f32[72,512]{1,0:T(8,128)S(1)}, u32[]{:S(2)}, u32[]{:S(2)}) %collective-permute-start.28) | collective-permute-done | bytes 147488 | tf_op jit(solution)/shard_map/ppermute | solution.py:236
  161.1 1.6 collective-permute-start.29
  164.2 2.1 %collective-permute-done.29.other_ref = f32[72,512]{1,0:T(8,128)S(1)} collective-permute-done((f32[72,512]{1,0:T(8,128)S(1)}, f32[72,512]{1,0:T(8,128)S(1)}, u32[]{:S(2)}, u32[]{:S(2)}) %collective-permute-start.29) | collective-permute-done | bytes 147488 | tf_op jit(solution)/shard_map/ppermute | solution.py:236
  169.3 3.4 %collective-permute-done.31 = f32[72,64]{1,0:T(8,128)S(1)} collective-permute-done((f32[72,64]{1,0:T(8,128)S(1)}, f32[72,64]{1,0:T(8,128)S(1)}, u32[]{:S(2)}, u32[]{:S(2)}) %collective-permute-start.31) | collective-permute-done | bytes 18464 | tf_op jit(solution)/shard_map/ppermute | solution.py:236
  172.8 1.6 collective-permute-start.32
  176.7 3.6 %collective-permute-done.33 = f32[8,64]{1,0:T(8,128)S(1)} collective-permute-done((f32[8,64]{1,0:T(8,128)S(1)}, f32[8,64]{1,0:T(8,128)S(1)}, u32[]{:S(2)}, u32[]{:S(2)}) %collective-permute-start.33) | collective-permute-done | bytes 2080 | tf_op jit(solution)/shard_map/ppermute | solution.py:236
  182.0 2.8 %collective-permute-done.34.other_ref = f32[8,64]{1,0:T(8,128)S(1)} collective-permute-done((f32[8,64]{1,0:T(8,128)S(1)}, f32[8,64]{1,0:T(8,128)S(1)}, u32[]{:S(2)}, u32[]{:S(2)}) %collective-permute-start.34) | collective-permute-done | bytes 2080 | tf_op jit(solution)/shard_map/ppermute | solution.py:236
  (90 shorter events, 37.5 us)
Async XLA Ops:
  0.6 1.0 copy-start
  1.9 1.4 collective-permute-start
  3.4 11.6 %collective-permute-start.1 = (f32[64,64]{1,0:T(8,128)S(1)}, f32[64,64]{1,0:T(8,128)S(1)}, u32[]{:S(2)}, u32[]{:S(2)}) collective-permute-start(f32[64,64]{1,0:T(8,128)S(1)} %add.78), channel_id=1, source_target_pairs={{0,2},{1,3},{2,0},{3,1},{4,6},{5,7},{6,4},{7,5},{8,10},{9,11},{10,... | collective-permute-start | bytes 49160 | tf_op jit(solution)/shard_map/ppermute | solution.py:236
  6.2 0.9 copy-start.1
  7.1 7.7 %copy-start.2 = (f32[8,64]{1,0:T(8,128)S(1)}, f32[8,64]{1,0:T(8,128)}, u32[]{:S(2)}) copy-start(f32[8,64]{1,0:T(8,128)} %time_ref.1) | copy-start | bytes 6148
  15.3 1.6 collective-permute-start.2
  16.9 8.4 %collective-permute-start.3 = (f32[64,1024]{1,0:T(8,128)S(1)}, f32[64,1024]{1,0:T(8,128)S(1)}, u32[]{:S(2)}, u32[]{:S(2)}) collective-permute-start(f32[64,1024]{1,0:T(8,128)S(1)} %add.80.mine_ref), channel_id=1, source_target_pairs={{0,2},{1,3},{2,0},{3,1},{4,6},{5,7},{6,4},{7,5},{8,10},{9,11},{10,... | collective-permute-start | bytes 786440 | tf_op jit(solution)/shard_map/ppermute | solution.py:236
  29.4 5.1 %collective-permute-start.4 = (f32[72,512]{1,0:T(8,128)S(1)}, f32[72,512]{1,0:T(8,128)S(1)}, u32[]{:S(2)}, u32[]{:S(2)}) collective-permute-start(f32[72,512]{1,0:T(8,128)S(1)} %get-tuple-element.58), channel_id=1, source_target_pairs={{0,4},{4,0},{8,12},{12,8},{16,20},{20,16},{24,28},{28,24},{1,5},{5... | collective-permute-start | bytes 442376 | tf_op jit(solution)/shard_map/ppermute | solution.py:236
  34.6 5.2 %collective-permute-start.5 = (f32[72,512]{1,0:T(8,128)S(1)}, f32[72,512]{1,0:T(8,128)S(1)}, u32[]{:S(2)}, u32[]{:S(2)}) collective-permute-start(f32[72,512]{1,0:T(8,128)S(1)} %add.81), channel_id=1, source_target_pairs={{0,8},{4,12},{8,0},{12,4},{16,24},{20,28},{24,16},{28,20},{1,9},{5... | collective-permute-start | bytes 442376 | tf_op jit(solution)/shard_map/ppermute | solution.py:236
  39.8 7.8 %collective-permute-start.6 = (f32[72,512]{1,0:T(8,128)S(1)}, f32[72,512]{1,0:T(8,128)S(1)}, u32[]{:S(2)}, u32[]{:S(2)}) collective-permute-start(f32[72,512]{1,0:T(8,128)S(1)} %add.82), channel_id=1, source_target_pairs={{0,16},{4,20},{8,24},{12,28},{16,0},{20,4},{24,8},{28,12},{1,17},{... | collective-permute-start | bytes 442376 | tf_op jit(solution)/shard_map/ppermute | solution.py:236
  47.7 5.2 %collective-permute-start.7 = (f32[72,512]{1,0:T(8,128)S(1)}, f32[72,512]{1,0:T(8,128)S(1)}, u32[]{:S(2)}, u32[]{:S(2)}) collective-permute-start(f32[72,512]{1,0:T(8,128)S(1)} %add.83.mine_ref), channel_id=1, source_target_pairs={{0,4},{4,0},{8,12},{12,8},{16,20},{20,16},{24,28},{28,24},{1,5},{5... | collective-permute-start | bytes 442376 | tf_op jit(solution)/shard_map/ppermute | solution.py:236
  54.0 1.3 collective-permute-start.8
  55.3 4.0 %collective-permute-start.9 = (f32[72,64]{1,0:T(8,128)S(1)}, f32[72,64]{1,0:T(8,128)S(1)}, u32[]{:S(2)}, u32[]{:S(2)}) collective-permute-start(f32[72,64]{1,0:T(8,128)S(1)} %add.84), channel_id=1, source_target_pairs={{0,2},{1,3},{2,0},{3,1},{4,6},{5,7},{6,4},{7,5},{8,10},{9,11},{10,... | collective-permute-start | bytes 55304 | tf_op jit(solution)/shard_map/ppermute | solution.py:236
  59.2 5.0 %collective-permute-start.10 = (f32[8,64]{1,0:T(8,128)S(1)}, f32[8,64]{1,0:T(8,128)S(1)}, u32[]{:S(2)}, u32[]{:S(2)}) collective-permute-start(f32[8,64]{1,0:T(8,128)S(1)} %slice.16), channel_id=1, source_target_pairs={{0,4},{4,0},{8,12},{12,8},{16,20},{20,16},{24,28},{28,24},{1,5},{5... | collective-permute-start | bytes 6152 | tf_op jit(solution)/shard_map/ppermute | solution.py:236
  64.3 3.7 %collective-permute-start.11 = (f32[8,64]{1,0:T(8,128)S(1)}, f32[8,64]{1,0:T(8,128)S(1)}, u32[]{:S(2)}, u32[]{:S(2)}) collective-permute-start(f32[8,64]{1,0:T(8,128)S(1)} %slice_add_fusion.2), channel_id=1, source_target_pairs={{0,8},{4,12},{8,0},{12,4},{16,24},{20,28},{24,16},{28,20},{1,9},{5... | collective-permute-start | bytes 6152 | tf_op jit(solution)/shard_map/ppermute | solution.py:236
  67.9 4.5 %collective-permute-start.12 = (f32[8,64]{1,0:T(8,128)S(1)}, f32[8,64]{1,0:T(8,128)S(1)}, u32[]{:S(2)}, u32[]{:S(2)}) collective-permute-start(f32[8,64]{1,0:T(8,128)S(1)} %add.87.mine_ref), channel_id=1, source_target_pairs={{0,16},{4,20},{8,24},{12,28},{16,0},{20,4},{24,8},{28,12},{1,17},{... | collective-permute-start | bytes 6152 | tf_op jit(solution)/shard_map/ppermute | solution.py:236
  72.9 1.6 collective-permute-start.13
  74.5 8.4 %collective-permute-start.14 = (f32[64,1024]{1,0:T(8,128)S(1)}, f32[64,1024]{1,0:T(8,128)S(1)}, u32[]{:S(2)}, u32[]{:S(2)}) collective-permute-start(f32[64,1024]{1,0:T(8,128)S(1)} %add.88.mine_ref), channel_id=1, source_target_pairs={{0,2},{1,3},{2,0},{3,1},{4,6},{5,7},{6,4},{7,5},{8,10},{9,11},{10,... | collective-permute-start | bytes 786440 | tf_op jit(solution)/shard_map/ppermute | solution.py:236
  87.1 5.1 %collective-permute-start.15 = (f32[72,512]{1,0:T(8,128)S(1)}, f32[72,512]{1,0:T(8,128)S(1)}, u32[]{:S(2)}, u32[]{:S(2)}) collective-permute-start(f32[72,512]{1,0:T(8,128)S(1)} %get-tuple-element.75), channel_id=1, source_target_pairs={{0,4},{4,0},{8,12},{12,8},{16,20},{20,16},{24,28},{28,24},{1,5},{5... | collective-permute-start | bytes 442376 | tf_op jit(solution)/shard_map/ppermute | solution.py:236
  92.2 5.2 %collective-permute-start.16 = (f32[72,512]{1,0:T(8,128)S(1)}, f32[72,512]{1,0:T(8,128)S(1)}, u32[]{:S(2)}, u32[]{:S(2)}) collective-permute-start(f32[72,512]{1,0:T(8,128)S(1)} %add.89), channel_id=1, source_target_pairs={{0,8},{4,12},{8,0},{12,4},{16,24},{20,28},{24,16},{28,20},{1,9},{5... | collective-permute-start | bytes 442376 | tf_op jit(solution)/shard_map/ppermute | solution.py:236
  97.5 7.7 %collective-permute-start.17 = (f32[72,512]{1,0:T(8,128)S(1)}, f32[72,512]{1,0:T(8,128)S(1)}, u32[]{:S(2)}, u32[]{:S(2)}) collective-permute-start(f32[72,512]{1,0:T(8,128)S(1)} %add.90), channel_id=1, source_target_pairs={{0,16},{4,20},{8,24},{12,28},{16,0},{20,4},{24,8},{28,12},{1,17},{... | collective-permute-start | bytes 442376 | tf_op jit(solution)/shard_map/ppermute | solution.py:236
  105.2 5.2 %collective-permute-start.18 = (f32[72,512]{1,0:T(8,128)S(1)}, f32[72,512]{1,0:T(8,128)S(1)}, u32[]{:S(2)}, u32[]{:S(2)}) collective-permute-start(f32[72,512]{1,0:T(8,128)S(1)} %add.91.mine_ref), channel_id=1, source_target_pairs={{0,4},{4,0},{8,12},{12,8},{16,20},{20,16},{24,28},{28,24},{1,5},{5... | collective-permute-start | bytes 442376 | tf_op jit(solution)/shard_map/ppermute | solution.py:236
  111.6 1.3 collective-permute-start.19
  112.8 4.0 %collective-permute-start.20 = (f32[72,64]{1,0:T(8,128)S(1)}, f32[72,64]{1,0:T(8,128)S(1)}, u32[]{:S(2)}, u32[]{:S(2)}) collective-permute-start(f32[72,64]{1,0:T(8,128)S(1)} %add.92), channel_id=1, source_target_pairs={{0,2},{1,3},{2,0},{3,1},{4,6},{5,7},{6,4},{7,5},{8,10},{9,11},{10,... | collective-permute-start | bytes 55304 | tf_op jit(solution)/shard_map/ppermute | solution.py:236
  116.8 3.8 %collective-permute-start.21 = (f32[8,64]{1,0:T(8,128)S(1)}, f32[8,64]{1,0:T(8,128)S(1)}, u32[]{:S(2)}, u32[]{:S(2)}) collective-permute-start(f32[8,64]{1,0:T(8,128)S(1)} %slice.17), channel_id=1, source_target_pairs={{0,4},{4,0},{8,12},{12,8},{16,20},{20,16},{24,28},{28,24},{1,5},{5... | collective-permute-start | bytes 6152 | tf_op jit(solution)/shard_map/ppermute | solution.py:236
  120.7 3.7 %collective-permute-start.22 = (f32[8,64]{1,0:T(8,128)S(1)}, f32[8,64]{1,0:T(8,128)S(1)}, u32[]{:S(2)}, u32[]{:S(2)}) collective-permute-start(f32[8,64]{1,0:T(8,128)S(1)} %slice_add_fusion.1), channel_id=1, source_target_pairs={{0,8},{4,12},{8,0},{12,4},{16,24},{20,28},{24,16},{28,20},{1,9},{5... | collective-permute-start | bytes 6152 | tf_op jit(solution)/shard_map/ppermute | solution.py:236
  124.3 4.5 %collective-permute-start.23 = (f32[8,64]{1,0:T(8,128)S(1)}, f32[8,64]{1,0:T(8,128)S(1)}, u32[]{:S(2)}, u32[]{:S(2)}) collective-permute-start(f32[8,64]{1,0:T(8,128)S(1)} %add.95.mine_ref), channel_id=1, source_target_pairs={{0,16},{4,20},{8,24},{12,28},{16,0},{20,4},{24,8},{28,12},{1,17},{... | collective-permute-start | bytes 6152 | tf_op jit(solution)/shard_map/ppermute | solution.py:236
  129.3 1.6 collective-permute-start.24
  131.0 8.4 %collective-permute-start.25 = (f32[64,1024]{1,0:T(8,128)S(1)}, f32[64,1024]{1,0:T(8,128)S(1)}, u32[]{:S(2)}, u32[]{:S(2)}) collective-permute-start(f32[64,1024]{1,0:T(8,128)S(1)} %add.96.mine_ref), channel_id=1, source_target_pairs={{0,2},{1,3},{2,0},{3,1},{4,6},{5,7},{6,4},{7,5},{8,10},{9,11},{10,... | collective-permute-start | bytes 786440 | tf_op jit(solution)/shard_map/ppermute | solution.py:236
  142.9 5.2 %collective-permute-start.26 = (f32[72,512]{1,0:T(8,128)S(1)}, f32[72,512]{1,0:T(8,128)S(1)}, u32[]{:S(2)}, u32[]{:S(2)}) collective-permute-start(f32[72,512]{1,0:T(8,128)S(1)} %get-tuple-element.93), channel_id=1, source_target_pairs={{0,4},{4,0},{8,12},{12,8},{16,20},{20,16},{24,28},{28,24},{1,5},{5... | collective-permute-start | bytes 442376 | tf_op jit(solution)/shard_map/ppermute | solution.py:236
  148.2 5.2 %collective-permute-start.27 = (f32[72,512]{1,0:T(8,128)S(1)}, f32[72,512]{1,0:T(8,128)S(1)}, u32[]{:S(2)}, u32[]{:S(2)}) collective-permute-start(f32[72,512]{1,0:T(8,128)S(1)} %add.97), channel_id=1, source_target_pairs={{0,8},{4,12},{8,0},{12,4},{16,24},{20,28},{24,16},{28,20},{1,9},{5... | collective-permute-start | bytes 442376 | tf_op jit(solution)/shard_map/ppermute | solution.py:236
  153.4 7.7 %collective-permute-start.28 = (f32[72,512]{1,0:T(8,128)S(1)}, f32[72,512]{1,0:T(8,128)S(1)}, u32[]{:S(2)}, u32[]{:S(2)}) collective-permute-start(f32[72,512]{1,0:T(8,128)S(1)} %add.98), channel_id=1, source_target_pairs={{0,16},{4,20},{8,24},{12,28},{16,0},{20,4},{24,8},{28,12},{1,17},{... | collective-permute-start | bytes 442376 | tf_op jit(solution)/shard_map/ppermute | solution.py:236
  161.1 5.2 %collective-permute-start.29 = (f32[72,512]{1,0:T(8,128)S(1)}, f32[72,512]{1,0:T(8,128)S(1)}, u32[]{:S(2)}, u32[]{:S(2)}) collective-permute-start(f32[72,512]{1,0:T(8,128)S(1)} %add.99.mine_ref), channel_id=1, source_target_pairs={{0,4},{4,0},{8,12},{12,8},{16,20},{20,16},{24,28},{28,24},{1,5},{5... | collective-permute-start | bytes 442376 | tf_op jit(solution)/shard_map/ppermute | solution.py:236
  167.5 1.3 collective-permute-start.30
  168.8 4.0 %collective-permute-start.31 = (f32[72,64]{1,0:T(8,128)S(1)}, f32[72,64]{1,0:T(8,128)S(1)}, u32[]{:S(2)}, u32[]{:S(2)}) collective-permute-start(f32[72,64]{1,0:T(8,128)S(1)} %add.100), channel_id=1, source_target_pairs={{0,2},{1,3},{2,0},{3,1},{4,6},{5,7},{6,4},{7,5},{8,10},{9,11},{10,... | collective-permute-start | bytes 55304 | tf_op jit(solution)/shard_map/ppermute | solution.py:236
  172.8 3.8 %collective-permute-start.32 = (f32[8,64]{1,0:T(8,128)S(1)}, f32[8,64]{1,0:T(8,128)S(1)}, u32[]{:S(2)}, u32[]{:S(2)}) collective-permute-start(f32[8,64]{1,0:T(8,128)S(1)} %slice.18), channel_id=1, source_target_pairs={{0,4},{4,0},{8,12},{12,8},{16,20},{20,16},{24,28},{28,24},{1,5},{5... | collective-permute-start | bytes 6152 | tf_op jit(solution)/shard_map/ppermute | solution.py:236
  176.6 3.7 %collective-permute-start.33 = (f32[8,64]{1,0:T(8,128)S(1)}, f32[8,64]{1,0:T(8,128)S(1)}, u32[]{:S(2)}, u32[]{:S(2)}) collective-permute-start(f32[8,64]{1,0:T(8,128)S(1)} %slice_add_fusion), channel_id=1, source_target_pairs={{0,8},{4,12},{8,0},{12,4},{16,24},{20,28},{24,16},{28,20},{1,9},{5... | collective-permute-start | bytes 6152 | tf_op jit(solution)/shard_map/ppermute | solution.py:236
  180.3 4.5 %collective-permute-start.34 = (f32[8,64]{1,0:T(8,128)S(1)}, f32[8,64]{1,0:T(8,128)S(1)}, u32[]{:S(2)}, u32[]{:S(2)}) collective-permute-start(f32[8,64]{1,0:T(8,128)S(1)} %add.103.mine_ref), channel_id=1, source_target_pairs={{0,16},{4,20},{8,24},{12,28},{16,0},{20,4},{24,8},{28,12},{1,17},{... | collective-permute-start | bytes 6152 | tf_op jit(solution)/shard_map/ppermute | solution.py:236
